TPU v7x, 32 devices: a 4x4x1 block of a 4x4x8 slice. The times are simulated.
32 devices in a mesh: dp: 1 (over z), ep: 32 (over x, y, core).
Axes of the slice: x: 4, y: 4, z: 1, core: 2. Of those that a mesh axis runs over, the one named last changes fastest.
The devices are a block of a 4x4x8 slice.
Arguments:
- x: bfloat16 [1, 32, 256, 2048], P('dp', 'ep')
- expert: int32 [1, 32, 256, 6], P('dp', 'ep')
- slot: int32 [1, 32, 256, 6], P('dp', 'ep')
- gate: float32 [1, 32, 256, 6], P('dp', 'ep')
- w_gate: bfloat16 [64, 2048, 1408], P('ep')
- w_up: bfloat16 [64, 2048, 1408], P('ep')
- w_down: bfloat16 [64, 1408, 2048], P('ep')
- s_gate: bfloat16 [2048, 2816], replicated
- s_up: bfloat16 [2048, 2816], replicated
- s_down: bfloat16 [2816, 2048], replicated
Outputs:
- y: bfloat16 [1, 32, 256, 2048], P('dp', 'ep')
All inputs are finite; a program needn't handle non-finite values.
Results may differ from a plain program's by a relative error of at most 0.009.
Values are sent between devices in bfloat16 or wider.
A program may use at most 768 MiB of HBM per device.

v0:
```python
import jax
import jax.numpy as jnp
from jax import lax
from jax.sharding import NamedSharding, PartitionSpec as P


def einsum(form, a, b):
    return jnp.einsum(form, a.astype(jnp.float32), b.astype(jnp.float32))


def for_all(x, s_gate, s_up, s_down):
    h = jax.nn.silu(einsum("...d,df->...f", x, s_gate)) * einsum("...d,df->...f", x, s_up)
    return einsum("...f,fd->...d", h.astype(jnp.bfloat16), s_down)


def solution(mesh):
    def placed(v, *spec):
        return lax.with_sharding_constraint(v, NamedSharding(mesh, P(*spec)))

    def step(x, expert, slot, gate, w_gate, w_up, w_down, s_gate, s_up, s_down):
        experts, (tokens, top) = w_gate.shape[0], expert.shape[2:]
        slots = 5 * tokens * top // (4 * experts)
        to_expert = jax.nn.one_hot(expert, experts, dtype=jnp.bfloat16)
        to_slot = jax.nn.one_hot(slot, slots, dtype=jnp.bfloat16)
        weighted = to_expert * gate[..., None].astype(jnp.bfloat16)
        dispatch = einsum("abtke,abtkc->abtec", to_expert, to_slot).astype(jnp.bfloat16)
        combine = einsum("abtke,abtkc->abtec", weighted, to_slot).astype(jnp.bfloat16)
        z = einsum("abtec,abtd->aebcd", dispatch, x).astype(jnp.bfloat16)
        z = placed(z, "dp", None, "ep", None, None)
        z = placed(z, "dp", "ep", None, None, None)
        h = jax.nn.silu(einsum("aebcd,edf->aebcf", z, w_gate))
        h = (h * einsum("aebcd,edf->aebcf", z, w_up)).astype(jnp.bfloat16)
        out = einsum("aebcf,efd->aebcd", h, w_down).astype(jnp.bfloat16)
        out = placed(out, "dp", "ep", None, None, None)
        out = placed(out, "dp", None, "ep", None, None)
        y = einsum("abtec,aebcd->abtd", combine, out)
        return (y + for_all(x, s_gate, s_up, s_down)).astype(jnp.bfloat16)

    return step
```

profile of v0, /device:TPU:105, one launch (start us, length us, event | category | flops | bytes accessed | tf_op | source)
XLA Modules:
  0.0 370.6 jit_solution(2827324600121925957)
XLA Ops:
  0.0 0.0 copy-start
  0.0 0.9 copy.30
  0.9 0.8 copy.32
  1.7 2.6 convolution_convert_fusion.1
  4.4 0.0 copy-done
  4.4 6.1 %convert_bitcast_fusion = bf16[1,64,1,30,2048]{4,1,3,2,0:T(8,128)(2,1)} fusion(bf16[256,64,30]{1,2,0:T(8,128)(2,1)S(1)} %convolution_convert_fusion.1, bf16[1,1,256,2048]{3,2,1,0:T(8,128)(2,1)S(1)} %copy-done), kind=kOutput, calls=%fused_computation.15 | convolution fusion | flops 2017198080 | bytes 9895936 | tf_op jit(solution)/abtec,abtd->aebcd/dot_general | solution.py:8
  10.5 13.4 %reshape.67 = bf16[1,32,2,1,30,2048]{5,2,1,4,3,0:T(2,128)(2,1)} reshape(bf16[1,64,1,30,2048]{4,1,3,2,0:T(8,128)(2,1)} %convert_bitcast_fusion) | data formatting | bytes 15728640 | tf_op jit(solution)/sharding_constraint;jit(solution)/sharding_constraint | solution.py:18
  23.9 9.4 %copy.22 = bf16[1,32,2,1,30,2048]{5,2,4,3,0,1:T(2,128)(2,1)S(1)} copy(bf16[1,32,2,1,30,2048]{5,2,1,4,3,0:T(2,128)(2,1)} %reshape.67) | data formatting | bytes 15728640 | tf_op jit(solution)/sharding_constraint;jit(solution)/sharding_constraint | solution.py:18
  33.4 101.3 %all-to-all.4 = bf16[1,32,2,1,30,2048]{5,2,4,3,0,1:T(2,128)(2,1)S(1)} all-to-all(bf16[1,32,2,1,30,2048]{5,2,4,3,0,1:T(2,128)(2,1)S(1)} %copy.22), channel_id=1, replica_groups=mesh['dp'=1,'ep'=32] {'ep'}, dimensions={1} | all-to-all | bytes 15728640 | tf_op jit(solution)/sharding_constraint;jit(solution)/sharding_constraint | solution.py:18
  134.7 0.0 copy-start.1
  134.7 3.2 copy-done.1
  137.8 30.1 %fusion.2 = f32[2,32,30,1408]{3,1,2,0:T(8,128)} fusion(bf16[2,2048,1408]{2,1,0:T(8,128)(2,1)} %param.5, bf16[1,32,2,1,30,2048]{5,2,4,3,0,1:T(2,128)(2,1)S(1)} %all-to-all.4), kind=kOutput, calls=%fused_computation.2 | convolution fusion | flops 11072962560 | bytes 30212096 | tf_op jit(solution)/aebcd,edf->aebcf/dot_general | solution.py:8
  168.0 27.6 %fusion.6 = bf16[1,2,32,30,1408]{4,2,3,1,0:T(8,128)(2,1)} fusion(f32[2,32,30,1408]{3,1,2,0:T(8,128)} %fusion.2, bf16[2,2048,1408]{2,1,0:T(8,128)(2,1)} %param.4, bf16[1,32,2,1,30,2048]{5,2,4,3,0,1:T(2,128)(2,1)} %copy-done.1), kind=kOutput, calls=%fused_computation.7 | convolution fusion | flops 11089182720 | bytes 35618816 | tf_op jit(solution)/aebcd,edf->aebcf/dot_general | solution.py:8
  195.6 16.8 %convert_bitcast_fusion.1 = bf16[1,2,32,1,30,2048]{5,2,4,1,3,0:T(8,128)(2,1)S(1)} fusion(bf16[2,1408,2048]{2,1,0:T(8,128)(2,1)} %param.6, bf16[1,2,32,30,1408]{4,2,3,1,0:T(8,128)(2,1)} %fusion.6), kind=kOutput, calls=%fused_computation.16 | convolution fusion | flops 11076894720 | bytes 24805376 | tf_op jit(solution)/aebcf,efd->aebcd/dot_general | solution.py:8
  212.4 9.0 %copy.24 = bf16[1,2,32,1,30,2048]{5,1,4,3,0,2:T(2,128)(2,1)} copy(bf16[1,2,32,1,30,2048]{5,2,4,1,3,0:T(8,128)(2,1)S(1)} %convert_bitcast_fusion.1) | data formatting | bytes 15728640 | tf_op jit(solution)/sharding_constraint;jit(solution)/sharding_constraint | solution.py:18
  221.4 0.0 copy-start.2
  221.4 11.2 %all-to-all-start.1 = ((bf16[1,2,32,1,30,2048]{5,1,4,3,0,2:T(2,128)(2,1)}), bf16[1,2,32,1,30,2048]{5,1,4,3,0,2:T(2,128)(2,1)}, u32[]{:S(2)}, u32[]{:S(2)}) async-start(bf16[1,2,32,1,30,2048]{5,1,4,3,0,2:T(2,128)(2,1)} %copy.24), calls=%async_computation.1 | async-start | bytes 15728640 | tf_op jit(solution)/sharding_constraint;jit(solution)/sharding_constraint | solution.py:18
  232.7 0.0 copy-done.2
  232.7 0.1 copy.31
  232.8 3.0 convolution_convert_fusion
  235.8 9.0 %convolution_bitcast_fusion.1 = f32[1,256,2816]{2,1,0:T(8,128)} fusion(bf16[2048,2816]{1,0:T(8,128)(2,1)} %param.7, bf16[1,1,256,2048]{3,2,1,0:T(8,128)(2,1)S(1)} %copy-done), kind=kOutput, calls=%fused_computation.22 | convolution fusion | flops 2952790016 | bytes 15466496 | tf_op jit(solution)/...d,df->...f/dot_general | solution.py:8
  244.8 15.9 %fusion.39 = f32[256,2048]{1,0:T(8,128)} fusion(bf16[2816,2048]{1,0:T(8,128)(2,1)} %param.9, bf16[2048,2816]{1,0:T(8,128)(2,1)} %param.8, f32[1,256,2816]{2,1,0:T(8,128)} %convolution_bitcast_fusion.1, bf16[1,1,256,2048]{3,2,1,0:T(8,128)(2,1)S(1)} %copy-done), kind=kOutput, calls=%fused_computation.41 | convolution fusion | flops 5909905408 | bytes 29097984 | tf_op jit(solution)/...f,fd->...d/dot_general | solution.py:8
  260.7 81.6 %all-to-all-done.1 = bf16[1,2,32,1,30,2048]{5,1,4,3,0,2:T(2,128)(2,1)} async-done(((bf16[1,2,32,1,30,2048]{5,1,4,3,0,2:T(2,128)(2,1)}), bf16[1,2,32,1,30,2048]{5,1,4,3,0,2:T(2,128)(2,1)}, u32[]{:S(2)}, u32[]{:S(2)}) %all-to-all-start.1) | async-done | bytes 7864352 | tf_op jit(solution)/sharding_constraint;jit(solution)/sharding_constraint | solution.py:18
  342.3 7.7 %copy.25 = bf16[1,32,2,1,30,2048]{5,2,1,4,3,0:T(2,128)(2,1)} copy(bf16[1,32,2,1,30,2048]{5,2,4,3,0,1:T(2,128)(2,1)} %bitcast.34) | data formatting | bytes 15728640 | tf_op jit(solution)/sharding_constraint;jit(solution)/sharding_constraint | solution.py:18
  350.0 12.4 %reshape.92 = bf16[64,30,2048]{2,0,1:T(8,128)(2,1)} reshape(bf16[1,32,2,1,30,2048]{5,2,1,4,3,0:T(2,128)(2,1)} %copy.25) | data formatting | bytes 15728640
  362.4 7.7 %fusion.26 = bf16[1,1,256,2048]{3,2,1,0:T(8,128)(2,1)} fusion(f32[256,2048]{1,0:T(8,128)} %fusion.39, bf16[64,30,2048]{2,0,1:T(8,128)(2,1)} %reshape.92, bf16[256,64,30]{1,2,0:T(8,128)(2,1)S(1)} %convolution_convert_fusion), kind=kOutput, calls=%fused_computation.28 | convolution fusion | flops 2014314496 | bytes 11993088 | tf_op jit(solution)/abtec,aebcd->abtd/dot_general | solution.py:8
  (1 shorter events, 0.0 us)
Async XLA Ops:
  0.0 4.4 %copy-start = (bf16[1,1,256,2048]{3,2,1,0:T(8,128)(2,1)S(1)}, bf16[1,1,256,2048]{3,2,1,0:T(8,128)(2,1)}, u32[]{:S(2)}) copy-start(bf16[1,1,256,2048]{3,2,1,0:T(8,128)(2,1)} %param.3) | copy-start | bytes 3145732
  134.7 3.2 copy-start.1
  221.4 11.3 %copy-start.2 = (f32[1,1,256,6]{2,1,3,0:T(1,128)S(1)}, f32[1,1,256,6]{2,1,3,0:T(1,128)}, u32[]{:S(2)}) copy-start(f32[1,1,256,6]{2,1,3,0:T(1,128)} %param.1) | copy-start | bytes 18436
  221.4 120.8 %all-to-all-start.1 = ((bf16[1,2,32,1,30,2048]{5,1,4,3,0,2:T(2,128)(2,1)}), bf16[1,2,32,1,30,2048]{5,1,4,3,0,2:T(2,128)(2,1)}, u32[]{:S(2)}, u32[]{:S(2)}) async-start(bf16[1,2,32,1,30,2048]{5,1,4,3,0,2:T(2,128)(2,1)} %copy.24), calls=%async_computation.1 | async-start | bytes 15728640 | tf_op jit(solution)/sharding_constraint;jit(solution)/sharding_constraint | solution.py:18
where the time goes:
time: 375 us; the launch traced here: 371 us
  matrix products  119 us (32%)
  blocking collectives  101 us (27%)
  waiting for transfers between devices  81.6 us (22%)
  local copies, waits for them, and re-layouts  57.1 us (15%)
  starting transfers between devices  11.2 us (3%)
    dot_general x9, matrix products, einsum(): return jnp.einsum(form, a.astype(jnp.float32), b.astype(jnp.float32))  119 us
    another operation x1, blocking collectives, placed(): return lax.with_sharding_constraint(v, NamedSharding(mesh, P(*spec)))  101 us
    another operation x1, waiting for transfers between devices, placed(): return lax.with_sharding_constraint(v, NamedSharding(mesh, P(*spec)))  81.6 us
    another operation x4, local copies, waits for them, and re-layouts, placed(): return lax.with_sharding_constraint(v, NamedSharding(mesh, P(*spec)))  39.6 us
    unnamed x7, local copies, waits for them, and re-layouts  15.6 us
    another operation x1, starting transfers between devices, placed(): return lax.with_sharding_constraint(v, NamedSharding(mesh, P(*spec)))  11.2 us
  transfers between devices with their start and end apart: 1, of which 1 were waited for; matrix products, arithmetic and copies ran while one was open for 8% of the time, Pallas kernels for 0%

commit v1 on v0

v1 whole, which is shorter than its diff:
```python
import contextlib
import functools
import math

import jax
import jax.numpy as jnp
from jax import lax
from jax.experimental import pallas as pl
from jax.experimental.pallas import tpu as pltpu
from jax.sharding import PartitionSpec as P

MESH = pl.DeviceIdType.MESH
OFFSETS = 4
HERE, ON, BACK, FAR = range(OFFSETS)
SAME, OTHER = range(2)
UNITS = ((HERE, SAME), (HERE, OTHER), (ON, SAME), (BACK, SAME), (ON, OTHER), (BACK, OTHER), (FAR, SAME), (FAR, OTHER))
LANE = 128
WIDE = 2 * LANE
BUFFERS = 6
COPIES = 33
BF16, F32 = jnp.bfloat16, jnp.float32
scope = contextlib.nullcontext


def dot(a, b):
    return jnp.dot(a, b, preferred_element_type=F32)


def swiglu(both):
    g, u = both[:, :LANE], both[:, LANE:]
    return (g * jax.nn.sigmoid(g) * u).astype(BF16)


def kernel(side, slots, x_hbm, expert_ref, slot_ref, gate_ref, wg, wu, wd, sg, su, sd, y_ref,
           xg, mg, column, onehot, combine, sent, fwd, z, r, fwdb, h, w, part, near, rfar, rn, ysh,
           in_sem, w_sem, send_sem, recv_sem):
    tokens, d = x_hbm.shape
    per, _, ff = wg.shape
    group = OFFSETS * slots
    unit = per * group
    rows = group + (-group) % 16
    last = unit - rows
    half = tokens // 2
    full = unit + (-unit) % LANE
    units = len(UNITS)
    total = units * full
    index = {u: k for k, u in enumerate(UNITS)}

    me = lax.axis_index("ep")
    core, chip = lax.rem(me, 2), lax.div(me, 2)
    py, px = lax.rem(chip, side), lax.div(chip, side)
    pa, pb = px + (py - px) * core, py + (px - py) * core
    sa, sb = 2 * side - (2 * side - 2) * core, 2 + (2 * side - 2) * core

    def at(da, db, other):
        a, b = lax.rem(pa + da + side, side), lax.rem(pb + db + side, side)
        return sa * a + sb * b + (1 - core if other else core)

    def copy(i, src, dst, to):
        return pltpu.make_async_remote_copy(
            src_ref=src, dst_ref=dst, send_sem=send_sem.at[i], recv_sem=recv_sem.at[i],
            device_id={"ep": to}, device_id_type=MESH)

    lo, hi, body = pl.ds(0, half), pl.ds(half, half), pl.ds(0, unit)
    c = {}

    def link(name, src, dst, to):
        c[name] = copy(len(c), src, dst, to)

    def back(i, j):
        return r.at[index[i, j], body]

    for i, way, first, second in ((ON, 1, lo, hi), (BACK, -1, hi, lo)):
        link(("x", i, 0), xg.at[HERE, first], xg.at[i, first], at(way, 0, SAME))
        link(("x", i, 1), xg.at[HERE, second], xg.at[i, second], at(way, 0, SAME))
        link(("m", i), mg.at[HERE], mg.at[i], at(way, 0, SAME))
        link(("xx", i), xg.at[i, first], xg.at[FAR, first], at(way, 0, SAME))
    link("mm", mg.at[ON], mg.at[FAR], at(1, 0, SAME))
    link(("z", HERE, OTHER), sent.at[HERE, OTHER], z.at[OTHER, HERE], at(0, 0, OTHER))
    link(("r", HERE, OTHER), z.at[OTHER, HERE], back(HERE, OTHER), at(0, 0, OTHER))
    for i, way in ((ON, 1), (BACK, -1)):
        for j in (SAME, OTHER):
            link(("z", i, j), sent.at[i, j], z.at[j, i], at(0, way, j))
        link(("r", i, SAME), z.at[SAME, i], back(i, SAME), at(0, -way, SAME))
        link(("r", i, OTHER), z.at[OTHER, i], back(i, OTHER), at(-way, 0, OTHER))
    for j, way in ((SAME, 1), (OTHER, -1)):
        link(("f", j), sent.at[FAR, j], fwd.at[j], at(0, way, SAME))
        link(("z", FAR, j), fwd.at[j], z.at[j, FAR], at(0, way, j))
        link(("r", FAR, j), fwdb.at[j], back(FAR, j), at(0, -way, SAME))
    link(("g", SAME), z.at[SAME, FAR], fwdb.at[SAME], at(0, -1, SAME))
    link(("g", OTHER), z.at[OTHER, FAR], fwdb.at[OTHER], at(1, 0, OTHER))
    for k, way, first, second in ((0, 1, lo, hi), (1, -1, hi, lo)):
        link(("pp", k), part.at[2, first], rfar.at[k], at(way, 0, SAME))
        link(("p", k, 0), part.at[k, second], rn.at[k, second], at(way, 0, SAME))
        link(("p", k, 1), part.at[k, first], rn.at[k, first], at(way, 0, SAME))
    assert len(c) == COPIES

    def start(*which):
        for i in which:
            c[i].start()

    def arrived(*which):
        for i in which:
            c[i].wait_recv()

    n_up, n_down, passes = ff // LANE, d // WIDE, 5
    n_tiles = n_up + n_down
    ahead = BUFFERS - 2
    assert per == 2 and n_up % 2 == 1 and n_down % 2 == 0

    def slot_of(p, t):
        return lax.rem(p * n_tiles + t, BUFFERS)

    def up_tile(p, t):
        slot = slot_of(p, t)
        out = []
        for e in range(per):
            for k, (shared, own) in enumerate(((sg, wg), (su, wu))):
                if p == 0:
                    src = shared.at[:, pl.ds(pl.multiple_of(e * ff + t * LANE, LANE), LANE)]
                else:
                    src = own.at[e, :, pl.ds(pl.multiple_of(t * LANE, LANE), LANE)]
                out.append(pltpu.make_async_copy(
                    src, w.at[slot, e, :, pl.ds(k * LANE, LANE)], w_sem.at[slot, len(out)]))
        return out

    def down_tile(p, t):
        slot = slot_of(p, t)
        cols = pl.ds(pl.multiple_of((t - n_up) * WIDE, WIDE), WIDE)
        out = []
        for e in range(per):
            src = sd.at[pl.ds(e * ff, ff), cols] if p == 0 else wd.at[e, :, cols]
            out.append(pltpu.make_async_copy(src, w.at[slot, e, pl.ds(0, ff), :], w_sem.at[slot, len(out)]))
        return out

    def go(copies):
        for one in copies:
            one.start()

    def done(copies):
        for one in copies:
            one.wait()

    def fetch_in_up(p, q):
        @pl.when(q < n_up)
        def _():
            go(up_tile(p, q))

        @pl.when(q >= n_up)
        def _():
            go(down_tile(p, q))

    def fetch_in_down(p, q):
        @pl.when(q < n_tiles)
        def _():
            go(down_tile(p, q))

        if p + 1 < passes:
            @pl.when(q >= n_tiles)
            def _():
                go(up_tile(p + 1, q - n_tiles))

    def ups(p, lhs):
        def some(ts):
            for t in ts:
                done(up_tile(p, t))
            for t in ts:
                fetch_in_up(p, t + ahead)
            for t in ts:
                for e in range(per):
                    v = swiglu(dot(lhs(e), w[slot_of(p, t), e]))
                    h[e, :, pl.ds(pl.multiple_of(t * LANE, LANE), LANE)] = v

        @pl.loop(0, n_up // 2)
        def _(i):
            some((2 * i, 2 * i + 1))

        some((jnp.int32(n_up - 1),))

    def downs(p, store):
        @pl.loop(0, n_down // 2)
        def _(i):
            ts = (n_up + 2 * i, n_up + 2 * i + 1)
            for t in ts:
                done(down_tile(p, t))
            for t in ts:
                fetch_in_down(p, t + ahead)
            for t in ts:
                cols = pl.ds(pl.multiple_of((t - n_up) * WIDE, WIDE), WIDE)
                store(cols, *(dot(h[e], w[slot_of(p, t), e, pl.ds(0, ff), :]) for e in range(per)))

    def expert_ups(p, a, b):
        def lhs(e):
            these = pl.ds(e * last, rows)
            return jnp.concatenate([z[*a, these, :], z[*b, these, :]], axis=0)
        ups(p, lhs)

    def expert_downs(p, a, b):
        def store(cols, first, second):
            for k, ref in enumerate((a, b)):
                v, u = (o[k * rows:(k + 1) * rows] for o in (first, second))
                row = lax.broadcasted_iota(jnp.int32, (rows - last, WIDE), 0)
                edge = jnp.where(row < group - last, v[last:], u[:rows - last])
                ref[pl.ds(0, last), cols] = v[:last].astype(BF16)
                ref[pl.ds(last, rows - last), cols] = edge.astype(BF16)
                ref[pl.ds(rows, last), cols] = u[rows - last:].astype(BF16)
        downs(p, store)

    def routing():
        def place(to, here):
            away = lax.rem(to - here + side, side)
            return away ^ lax.shift_right_logical(away, 1)

        tos, spots, numbers = [], [], []
        number = lax.broadcasted_iota(jnp.int32, (1, tokens), 1).astype(F32) + 1.0
        n_to = OFFSETS * units
        for k in range(expert_ref.shape[0]):
            expert, slot = expert_ref[k], slot_ref[k]
            device, e = lax.div(expert, per), lax.rem(expert, per)
            other = lax.rem(device, 2) ^ core
            chip_to = lax.div(device, 2)
            ty, tx = lax.rem(chip_to, side), lax.div(chip_to, side)
            ta, tb = tx + (ty - tx) * core, ty + (tx - ty) * core
            oa, ob = place(ta, pa), place(tb, pb)
            u = jnp.where(ob == HERE, other, jnp.where(ob == FAR, index[FAR, SAME] + other, ob + 1 + 2 * other))
            to = u * OFFSETS + oa
            spot = jnp.where(slot < slots, (e * OFFSETS + oa) * slots + slot, -1)
            tos.append(jnp.where(lax.broadcasted_iota(jnp.int32, (n_to, tokens), 0) == to, 1.0, 0.0).astype(BF16))
            hit = lax.broadcasted_iota(jnp.int32, (full, tokens), 0) == spot
            spots.append(jnp.where(hit, number, 0.0).astype(BF16))
            numbers.append(jnp.where(hit, gate_ref[k], 0.0).astype(BF16))
        a = jnp.concatenate(tos, axis=1)
        for base, b in ((0, spots), (OFFSETS, numbers)):
            found = lax.dot_general(a, jnp.concatenate(b, axis=1), (((1,), (1,)), ((), ())),
                                    preferred_element_type=F32)
            for u in range(units):
                mg[HERE, pl.ds(base, OFFSETS), pl.ds(u * full, full)] = found[u * OFFSETS:(u + 1) * OFFSETS]

    x_in = pltpu.make_async_copy(x_hbm, xg.at[HERE], in_sem.at[0])
    with scope("enter"):
        x_in.start()
        for t in range(ahead):
            go(up_tile(0, t))
        barrier = pltpu.get_barrier_semaphore()
        peers = [at(da, db, j) for da, db in ((1, 0), (-1, 0), (0, 1), (0, -1)) for j in (SAME, OTHER)]
        peers.append(at(0, 0, OTHER))
        for peer in peers:
            pl.semaphore_signal(barrier, inc=1, device_id={"ep": peer}, device_id_type=MESH)
    with scope("routing"):
        routing()
        if full > unit:
            r[:, pl.ds(unit, full - unit), :] = jnp.zeros((units, full - unit, d), BF16)
    with scope("x_in"):
        x_in.wait()
        pl.semaphore_wait(barrier, len(peers))
        for k in range(2):
            start(("x", ON, k), ("x", BACK, k))
        start(("m", ON), ("m", BACK))

    with scope("shared_up"):
        ups(0, lambda e: xg[HERE])

    def shared_store(cols, first, second):
        ysh[:, cols] = first + second

    with scope("x_wait"):
        for i in (ON, BACK):
            arrived(("x", i, 0))
            start(("xx", i))
    with scope("shared_down"):
        downs(0, shared_store)
    with scope("xx_wait"):
        for i in (ON, BACK):
            arrived(("x", i, 1), ("m", i))
        start("mm")
        arrived(("xx", ON), ("xx", BACK), "mm")

    def table(s, base=0):
        return mg[s, s + base:s + base + 1, :]

    with scope("tables"):
        merged = jnp.zeros(mg.shape[1:], F32)
        row = lax.broadcasted_iota(jnp.int32, merged.shape, 0)
        for s in range(OFFSETS):
            merged = jnp.where(row == s, mg[s], merged)
        column[...] = jnp.transpose(merged)

    step = min(d, 8 * LANE)

    def gather(i, j, out):
        begin = index[i, j] * full
        lane = lax.broadcasted_iota(jnp.int32, (unit, tokens), 1).astype(F32) + 1.0
        for s in range(OFFSETS):
            token = column[pl.ds(begin, unit), s:s + 1]
            onehot[:, pl.ds(s * tokens, tokens)] = jnp.where(lane == token, 1.0, 0.0).astype(BF16)

        @pl.loop(0, d // step)
        def _(k):
            cols = pl.ds(pl.multiple_of(k * step, step), step)
            out[:, cols] = dot(onehot[...], xg[:, :, cols].reshape(OFFSETS * tokens, step)).astype(BF16)

    def gather_and_send(i, j):
        with scope("gather"):
            gather(i, j, sent.at[i, j])
        start(("f", j) if i == FAR else ("z", i, j))

    gather_and_send(FAR, SAME)
    gather_and_send(FAR, OTHER)
    gather_and_send(ON, SAME)
    gather_and_send(BACK, SAME)
    gather_and_send(HERE, OTHER)
    with scope("gather"):
        gather(HERE, SAME, z.at[SAME, HERE])
        gather(ON, OTHER, sent.at[ON, OTHER])
        gather(BACK, OTHER, sent.at[BACK, OTHER])
    with scope("wait_f"):
        for j in (SAME, OTHER):
            arrived(("f", j))
            start(("z", FAR, j))
    start(("z", ON, OTHER), ("z", BACK, OTHER))

    with scope("wait_here"):
        arrived(("z", HERE, OTHER))
    with scope("ffn_here"):
        expert_ups(1, (SAME, HERE), (OTHER, HERE))
        expert_downs(1, r.at[index[HERE, SAME]], z.at[OTHER, HERE])
    start(("r", HERE, OTHER))
    with scope("wait_same"):
        arrived(("z", ON, SAME), ("z", BACK, SAME))
    with scope("ffn_same"):
        expert_ups(2, (SAME, ON), (SAME, BACK))
        expert_downs(2, z.at[SAME, ON], z.at[SAME, BACK])
    start(("r", ON, SAME), ("r", BACK, SAME))
    with scope("wait_far"):
        arrived(("z", FAR, SAME), ("z", FAR, OTHER))
    with scope("ffn_far"):
        expert_ups(3, (SAME, FAR), (OTHER, FAR))
        expert_downs(3, z.at[SAME, FAR], z.at[OTHER, FAR])
    start(("g", SAME), ("g", OTHER))
    with scope("wait_other"):
        arrived(("z", ON, OTHER), ("z", BACK, OTHER))
    with scope("ffn_other_up"):
        expert_ups(4, (OTHER, ON), (OTHER, BACK))
    with scope("ffn_other_down"):
        expert_downs(4, z.at[OTHER, ON], z.at[OTHER, BACK])
    start(("r", ON, OTHER), ("r", BACK, OTHER))
    with scope("wait_g"):
        for j in (SAME, OTHER):
            arrived(("g", j))
            start(("r", FAR, j))
    with scope("wait_r_near"):
        arrived(*(("r", i, j) for i, j in UNITS[1:] if i != FAR))
    with scope("wait_r_far"):
        arrived(("r", FAR, SAME), ("r", FAR, OTHER))

    def add_up(s, store):
        token = lax.broadcasted_iota(jnp.int32, (tokens, total), 0).astype(F32) + 1.0
        combine[...] = jnp.where(token == table(s), table(s, OFFSETS), 0.0).astype(BF16)

        @pl.loop(0, d // step)
        def _(k):
            cols = pl.ds(pl.multiple_of(k * step, step), step)
            store(cols, dot(combine[...], r[:, :, cols].reshape(total, step)))

    def keep_far(cols, o):
        part[2, :, cols] = o.astype(BF16)

    def keep_next(cols, o):
        near[0, :, cols] = o[:half]
        part[0, hi, cols] = o[half:].astype(BF16)

    def keep_back(cols, o):
        near[1, :, cols] = o[half:]
        part[1, lo, cols] = o[:half].astype(BF16)

    def keep_own(cols, o):
        ysh[:, cols] = ysh[:, cols] + o

    with scope("sum_far"):
        add_up(FAR, keep_far)
    start(("pp", 0), ("pp", 1))
    with scope("sum_near"):
        add_up(BACK, keep_next)
        start(("p", 0, 0))
        add_up(ON, keep_back)
        start(("p", 1, 0))
    with scope("wait_pp"):
        for k, first in ((0, lo), (1, hi)):
            arrived(("pp", k))
            part[k, first, :] = (near[k] + rfar[k].astype(F32)).astype(BF16)
            start(("p", k, 1))
    with scope("sum_own"):
        add_up(HERE, keep_own)
    with scope("wait_p"):
        arrived(*(("p", k, v) for k in range(2) for v in range(2)))
    with scope("leave"):
        y_ref[...] = (ysh[...] + (rn[0].astype(F32) + rn[1].astype(F32))).astype(y_ref.dtype)
        for one in c.values():
            one.wait_send()


def solution(mesh):
    side = math.isqrt(mesh.shape["ep"] // 2)
    assert side == OFFSETS

    def local(x, expert, slot, gate, w_gate, w_up, w_down, s_gate, s_up, s_down):
        tokens, d = x.shape[2:]
        top = expert.shape[3]
        per, _, ff = w_gate.shape
        experts = per * mesh.shape["ep"]
        slots = 5 * tokens * top // (4 * experts)
        unit = per * OFFSETS * slots
        full = unit + (-unit) % LANE
        half, units = tokens // 2, len(UNITS)
        choices = (v.reshape(tokens, top).T.reshape(top, 1, tokens) for v in (expert, slot, gate))
        anywhere, vmem = pl.BlockSpec(memory_space=pl.ANY), pl.BlockSpec(memory_space=pltpu.VMEM)
        y = pl.pallas_call(
            functools.partial(kernel, side, slots),
            out_shape=jax.ShapeDtypeStruct((tokens, d), x.dtype),
            in_specs=[anywhere] + [vmem] * 3 + [anywhere] * 6,
            out_specs=vmem,
            scratch_shapes=[
                pltpu.VMEM((OFFSETS, tokens, d), BF16),
                pltpu.VMEM((OFFSETS, 2 * OFFSETS, units * full), F32),
                pltpu.VMEM((units * full, 2 * OFFSETS), F32),
                pltpu.VMEM((unit, OFFSETS * tokens), BF16),
                pltpu.VMEM((tokens, units * full), BF16),
                pltpu.VMEM((OFFSETS, 2, unit, d), BF16),
                pltpu.VMEM((2, unit, d), BF16),
                pltpu.VMEM((2, OFFSETS, unit, d), BF16),
                pltpu.VMEM((units, full, d), BF16),
                pltpu.VMEM((2, unit, d), BF16),
                pltpu.VMEM((per, 2 * (unit // per + 8), ff), BF16),
                pltpu.VMEM((BUFFERS, per, d, WIDE), BF16),
                pltpu.VMEM((3, tokens, d), BF16),
                pltpu.VMEM((2, half, d), F32),
                pltpu.VMEM((2, half, d), BF16),
                pltpu.VMEM((2, tokens, d), BF16),
                pltpu.VMEM((tokens, d), F32),
                pltpu.SemaphoreType.DMA((1,)),
                pltpu.SemaphoreType.DMA((BUFFERS, 4)),
                pltpu.SemaphoreType.DMA((COPIES,)),
                pltpu.SemaphoreType.DMA((COPIES,)),
            ],
            compiler_params=pltpu.CompilerParams(
                collective_id=0, has_side_effects=True, vmem_limit_bytes=67_000_000),
            name="moe",
        )(x.reshape(tokens, d), *choices, w_gate, w_up, w_down, s_gate, s_up, s_down)
        return y.reshape(x.shape)

    spread, held, whole = P("dp", "ep", None, None), P("ep", None, None), P(None, None)
    return jax.shard_map(
        local, mesh=mesh, in_specs=(spread,) * 4 + (held,) * 3 + (whole,) * 3, out_specs=spread, check_vma=False)
```

time: 375 us -> 150 us (0.40)
  the two profiles are of different devices: /device:TPU:105 before, /device:TPU:98 now
where the time goes in v1:
time: 150 us
  Pallas kernels  144 us (96%)
  local copies, waits for them, and re-layouts  6.18 us (4%)
    pallas_call x1, Pallas kernels, local(): pl.pallas_call(functools.partial(kernel, side, slots), out_shape=jax.Shap...  144 us
    unnamed x4, local copies, waits for them, and re-layouts  4.38 us

profile of v1, /device:TPU:98, one launch (start us, length us, event | category | flops | bytes accessed | tf_op | source)
XLA Modules:
  0.0 149.7 jit_solution(16671680093164460770)
XLA Ops:
  0.0 0.7 copy.19
  0.7 0.6 reshape.26.expert_ref
  1.3 0.7 copy.18
  2.0 0.6 reshape.28.slot_ref
  2.6 0.7 copy.17
  3.3 0.6 reshape.30.gate_ref
  3.9 143.5 %moe.1 = bf16[256,2048]{1,0:T(8,128)(2,1)} custom-call(bf16[256,2048]{1,0:T(8,128)(2,1)} %bitcast.18, s32[6,1,256]{2,1,0:T(1,128)} %reshape.26.expert_ref, s32[6,1,256]{2,1,0:T(1,128)} %reshape.28.slot_ref, f32[6,1,256]{2,1,0:T(1,128)} %reshape.30.gate_ref, bf16[2,2048,1408]{2,1,0:T(8,128)(2,1)} %wg.1, bf16[2,2048,1408]{2,1,0:T(8,128)(2,1)} %wu.1, ...), custom_call_target="tpu_custom_call" | custom-call | tf_op jit(solution)/shard_map/moe/pallas_call | solution.py:417
  147.4 2.3 %copy.21 = bf16[1,1,256,2048]{3,2,1,0:T(8,128)(2,1)} copy(bf16[1,1,256,2048]{3,2,1,0:T(8,128)(2,1)} %bitcast.17) | data formatting | bytes 2097152

commit v2 on v1

--- a/solution.py
+++ b/solution.py
@@ -17,7 +17,7 @@
 LANE = 128
 WIDE = 2 * LANE
 BUFFERS = 6
-COPIES = 33
+COPIES = 34
 BF16, F32 = jnp.bfloat16, jnp.float32
 scope = contextlib.nullcontext
 
@@ -31,8 +31,8 @@
     return (g * jax.nn.sigmoid(g) * u).astype(BF16)
 
 
-def kernel(side, slots, x_hbm, expert_ref, slot_ref, gate_ref, wg, wu, wd, sg, su, sd, y_ref,
-           xg, mg, column, onehot, combine, sent, fwd, z, r, fwdb, h, w, part, near, rfar, rn, ysh,
+def kernel(side, slots, x_hbm, expert_hbm, slot_hbm, gate_hbm, wg, wu, wd, sg, su, sd, y_ref,
+           expert_ref, slot_ref, gate_ref, xg, mg, column, onehot, combine, sent, fwd, z, r, fwdb, h, w, part, near, rfar, rn, ysh,
            in_sem, w_sem, send_sem, recv_sem):
     tokens, d = x_hbm.shape
     per, _, ff = wg.shape
@@ -73,9 +73,10 @@
     for i, way, first, second in ((ON, 1, lo, hi), (BACK, -1, hi, lo)):
         link(("x", i, 0), xg.at[HERE, first], xg.at[i, first], at(way, 0, SAME))
         link(("x", i, 1), xg.at[HERE, second], xg.at[i, second], at(way, 0, SAME))
-        link(("m", i), mg.at[HERE], mg.at[i], at(way, 0, SAME))
+        link(("m", i), mg.at[HERE, i], mg.at[i, i], at(way, 0, SAME))
         link(("xx", i), xg.at[i, first], xg.at[FAR, first], at(way, 0, SAME))
-    link("mm", mg.at[ON], mg.at[FAR], at(1, 0, SAME))
+    link(("m", FAR), mg.at[HERE, FAR], mg.at[ON, FAR], at(1, 0, SAME))
+    link("mm", mg.at[ON, FAR], mg.at[FAR, FAR], at(1, 0, SAME))
     link(("z", HERE, OTHER), sent.at[HERE, OTHER], z.at[OTHER, HERE], at(0, 0, OTHER))
     link(("r", HERE, OTHER), z.at[OTHER, HERE], back(HERE, OTHER), at(0, 0, OTHER))
     for i, way in ((ON, 1), (BACK, -1)):
@@ -230,32 +231,36 @@
             spots.append(jnp.where(hit, number, 0.0).astype(BF16))
             numbers.append(jnp.where(hit, gate_ref[k], 0.0).astype(BF16))
         a = jnp.concatenate(tos, axis=1)
-        for base, b in ((0, spots), (OFFSETS, numbers)):
+        for v, b in enumerate((spots, numbers)):
             found = lax.dot_general(a, jnp.concatenate(b, axis=1), (((1,), (1,)), ((), ())),
                                     preferred_element_type=F32)
             for u in range(units):
-                mg[HERE, pl.ds(base, OFFSETS), pl.ds(u * full, full)] = found[u * OFFSETS:(u + 1) * OFFSETS]
-
-    x_in = pltpu.make_async_copy(x_hbm, xg.at[HERE], in_sem.at[0])
+                for oa in range(OFFSETS):
+                    k = u * OFFSETS + oa
+                    mg[HERE, oa, v:v + 1, pl.ds(u * full, full)] = found[k:k + 1]
+
+    inputs = [
+        pltpu.make_async_copy(src, dst, in_sem.at[k]) for k, (src, dst) in enumerate((
+            (x_hbm, xg.at[HERE]), (expert_hbm, expert_ref), (slot_hbm, slot_ref), (gate_hbm, gate_ref)))]
     with scope("enter"):
-        x_in.start()
-        for t in range(ahead):
-            go(up_tile(0, t))
+        go(inputs)
         barrier = pltpu.get_barrier_semaphore()
         peers = [at(da, db, j) for da, db in ((1, 0), (-1, 0), (0, 1), (0, -1)) for j in (SAME, OTHER)]
         peers.append(at(0, 0, OTHER))
         for peer in peers:
             pl.semaphore_signal(barrier, inc=1, device_id={"ep": peer}, device_id_type=MESH)
+    with scope("x_in"):
+        done(inputs)
+        pl.semaphore_wait(barrier, len(peers))
+        for k in range(2):
+            start(("x", ON, k), ("x", BACK, k))
+        for t in range(ahead):
+            go(up_tile(0, t))
     with scope("routing"):
         routing()
         if full > unit:
             r[:, pl.ds(unit, full - unit), :] = jnp.zeros((units, full - unit, d), BF16)
-    with scope("x_in"):
-        x_in.wait()
-        pl.semaphore_wait(barrier, len(peers))
-        for k in range(2):
-            start(("x", ON, k), ("x", BACK, k))
-        start(("m", ON), ("m", BACK))
+        start(("m", ON), ("m", BACK), ("m", FAR))
 
     with scope("shared_up"):
         ups(0, lambda e: xg[HERE])
@@ -267,62 +272,72 @@
         for i in (ON, BACK):
             arrived(("x", i, 0))
             start(("xx", i))
+        arrived(("m", FAR))
+        start("mm")
     with scope("shared_down"):
         downs(0, shared_store)
-    with scope("xx_wait"):
+    with scope("x_rest"):
         for i in (ON, BACK):
             arrived(("x", i, 1), ("m", i))
-        start("mm")
-        arrived(("xx", ON), ("xx", BACK), "mm")
-
-    def table(s, base=0):
-        return mg[s, s + base:s + base + 1, :]
-
-    with scope("tables"):
-        merged = jnp.zeros(mg.shape[1:], F32)
+
+    def table(s, v=0):
+        return mg[s, s, v:v + 1, :]
+
+    def tables(sources):
+        merged = jnp.zeros((2 * OFFSETS, total), F32)
         row = lax.broadcasted_iota(jnp.int32, merged.shape, 0)
-        for s in range(OFFSETS):
-            merged = jnp.where(row == s, mg[s], merged)
+        for s in sources:
+            merged = jnp.where(row == s, table(s), merged)
         column[...] = jnp.transpose(merged)
 
     step = min(d, 8 * LANE)
 
-    def gather(i, j, out):
+    def gather(i, j, out, first=HERE, end=OFFSETS):
         begin = index[i, j] * full
         lane = lax.broadcasted_iota(jnp.int32, (unit, tokens), 1).astype(F32) + 1.0
-        for s in range(OFFSETS):
+        for s in range(first, end):
             token = column[pl.ds(begin, unit), s:s + 1]
             onehot[:, pl.ds(s * tokens, tokens)] = jnp.where(lane == token, 1.0, 0.0).astype(BF16)
+        these = pl.ds(first * tokens, (end - first) * tokens)
 
         @pl.loop(0, d // step)
         def _(k):
             cols = pl.ds(pl.multiple_of(k * step, step), step)
-            out[:, cols] = dot(onehot[...], xg[:, :, cols].reshape(OFFSETS * tokens, step)).astype(BF16)
-
-    def gather_and_send(i, j):
-        with scope("gather"):
-            gather(i, j, sent.at[i, j])
+            v = dot(onehot[:, these], xg[first:end, :, cols].reshape((end - first) * tokens, step))
+            if first > HERE:
+                v = v + out[:, cols].astype(F32)
+            out[:, cols] = v.astype(BF16)
+
+    early = ((FAR, SAME), (FAR, OTHER), (ON, SAME), (BACK, SAME))
+    with scope("gather_early"):
+        tables((HERE, ON, BACK))
+        for i, j in early:
+            gather(i, j, sent.at[i, j], end=FAR)
+    with scope("xx_wait"):
+        arrived(("xx", ON), ("xx", BACK), "mm")
+    with scope("tables"):
+        tables(range(OFFSETS))
+    for i, j in early:
+        with scope("gather_far"):
+            gather(i, j, sent.at[i, j], first=FAR)
         start(("f", j) if i == FAR else ("z", i, j))
-
-    gather_and_send(FAR, SAME)
-    gather_and_send(FAR, OTHER)
-    gather_and_send(ON, SAME)
-    gather_and_send(BACK, SAME)
-    gather_and_send(HERE, OTHER)
     with scope("gather"):
+        gather(HERE, OTHER, sent.at[HERE, OTHER])
+        start(("z", HERE, OTHER))
         gather(HERE, SAME, z.at[SAME, HERE])
         gather(ON, OTHER, sent.at[ON, OTHER])
         gather(BACK, OTHER, sent.at[BACK, OTHER])
+
+    with scope("wait_here"):
+        arrived(("z", HERE, OTHER))
+    with scope("ffn_here_up"):
+        expert_ups(1, (SAME, HERE), (OTHER, HERE))
     with scope("wait_f"):
         for j in (SAME, OTHER):
             arrived(("f", j))
             start(("z", FAR, j))
     start(("z", ON, OTHER), ("z", BACK, OTHER))
-
-    with scope("wait_here"):
-        arrived(("z", HERE, OTHER))
-    with scope("ffn_here"):
-        expert_ups(1, (SAME, HERE), (OTHER, HERE))
+    with scope("ffn_here_down"):
         expert_downs(1, r.at[index[HERE, SAME]], z.at[OTHER, HERE])
     start(("r", HERE, OTHER))
     with scope("wait_same"):
@@ -350,20 +365,26 @@
             start(("r", FAR, j))
     with scope("wait_r_near"):
         arrived(*(("r", i, j) for i, j in UNITS[1:] if i != FAR))
-    with scope("wait_r_far"):
-        arrived(("r", FAR, SAME), ("r", FAR, OTHER))
-
-    def add_up(s, store):
+
+    def weigh(s):
         token = lax.broadcasted_iota(jnp.int32, (tokens, total), 0).astype(F32) + 1.0
-        combine[...] = jnp.where(token == table(s), table(s, OFFSETS), 0.0).astype(BF16)
+        combine[...] = jnp.where(token == table(s), table(s, 1), 0.0).astype(BF16)
+
+    def add_up(store, first=0, end=units):
+        these = pl.ds(first * full, (end - first) * full)
 
         @pl.loop(0, d // step)
         def _(k):
             cols = pl.ds(pl.multiple_of(k * step, step), step)
-            store(cols, dot(combine[...], r[:, :, cols].reshape(total, step)))
+            store(cols, dot(combine[:, these], r[first:end, :, cols].reshape((end - first) * full, step)))
+
+    def begin_far(cols, o):
+        near[0, :, cols] = o[:half]
+        near[1, :, cols] = o[half:]
 
     def keep_far(cols, o):
-        part[2, :, cols] = o.astype(BF16)
+        part[2, lo, cols] = (near[0, :, cols] + o[:half]).astype(BF16)
+        part[2, hi, cols] = (near[1, :, cols] + o[half:]).astype(BF16)
 
     def keep_next(cols, o):
         near[0, :, cols] = o[:half]
@@ -376,13 +397,20 @@
     def keep_own(cols, o):
         ysh[:, cols] = ysh[:, cols] + o
 
+    with scope("sum_far_early"):
+        weigh(FAR)
+        add_up(begin_far, end=index[FAR, SAME])
+    with scope("wait_r_far"):
+        arrived(("r", FAR, SAME), ("r", FAR, OTHER))
     with scope("sum_far"):
-        add_up(FAR, keep_far)
+        add_up(keep_far, first=index[FAR, SAME])
     start(("pp", 0), ("pp", 1))
     with scope("sum_near"):
-        add_up(BACK, keep_next)
+        weigh(BACK)
+        add_up(keep_next)
         start(("p", 0, 0))
-        add_up(ON, keep_back)
+        weigh(ON)
+        add_up(keep_back)
         start(("p", 1, 0))
     with scope("wait_pp"):
         for k, first in ((0, lo), (1, hi)):
@@ -390,7 +418,8 @@
             part[k, first, :] = (near[k] + rfar[k].astype(F32)).astype(BF16)
             start(("p", k, 1))
     with scope("sum_own"):
-        add_up(HERE, keep_own)
+        weigh(HERE)
+        add_up(keep_own)
     with scope("wait_p"):
         arrived(*(("p", k, v) for k in range(2) for v in range(2)))
     with scope("leave"):
@@ -412,16 +441,17 @@
         unit = per * OFFSETS * slots
         full = unit + (-unit) % LANE
         half, units = tokens // 2, len(UNITS)
-        choices = (v.reshape(tokens, top).T.reshape(top, 1, tokens) for v in (expert, slot, gate))
+        choices = (v.transpose(0, 3, 1, 2).reshape(top, 1, tokens) for v in (expert, slot, gate))
         anywhere, vmem = pl.BlockSpec(memory_space=pl.ANY), pl.BlockSpec(memory_space=pltpu.VMEM)
         y = pl.pallas_call(
             functools.partial(kernel, side, slots),
             out_shape=jax.ShapeDtypeStruct((tokens, d), x.dtype),
-            in_specs=[anywhere] + [vmem] * 3 + [anywhere] * 6,
+            in_specs=[anywhere] * 10,
             out_specs=vmem,
             scratch_shapes=[
+                *(pltpu.VMEM((top, 1, tokens), v.dtype) for v in (expert, slot, gate)),
                 pltpu.VMEM((OFFSETS, tokens, d), BF16),
-                pltpu.VMEM((OFFSETS, 2 * OFFSETS, units * full), F32),
+                pltpu.VMEM((OFFSETS, OFFSETS, 2, units * full), F32),
                 pltpu.VMEM((units * full, 2 * OFFSETS), F32),
                 pltpu.VMEM((unit, OFFSETS * tokens), BF16),
                 pltpu.VMEM((tokens, units * full), BF16),
@@ -437,7 +467,7 @@
                 pltpu.VMEM((2, half, d), BF16),
                 pltpu.VMEM((2, tokens, d), BF16),
                 pltpu.VMEM((tokens, d), F32),
-                pltpu.SemaphoreType.DMA((1,)),
+                pltpu.SemaphoreType.DMA((4,)),
                 pltpu.SemaphoreType.DMA((BUFFERS, 4)),
                 pltpu.SemaphoreType.DMA((COPIES,)),
                 pltpu.SemaphoreType.DMA((COPIES,)),

time: 150 us -> 143 us (0.953)
  local copies, waits for them, and re-layouts: 6.18 us -> 2.3 us
  Pallas kernels: 144 us -> 141 us
    pallas_call x1, Pallas kernels: 144 us -> 141 us  [local(): pl.pallas_call(functools.partial(kernel, side, slots), out_shape=jax.Shap...]
    unnamed x4 -> x1, local copies, waits for them, and re-layouts: 4.38 us -> 2.3 us
    reshape x3 -> x0, local copies, waits for them, and re-layouts: 1.8 us -> none  [local(): v.reshape(tokens, top).T.reshape(top, 1, tokens)]
where the time goes in v2:
time: 143 us
  Pallas kernels  141 us (99%)
  local copies, waits for them, and re-layouts  2.3 us (2%)
    pallas_call x1, Pallas kernels, local(): pl.pallas_call(functools.partial(kernel, side, slots), out_shape=jax.Shap...  141 us

profile of v2, /device:TPU:98, one launch (start us, length us, event | category | flops | bytes accessed | tf_op | source)
XLA Modules:
  0.0 142.9 jit_solution(8568697278319863788)
XLA Ops:
  0.0 140.6 %moe.1 = bf16[256,2048]{1,0:T(8,128)(2,1)} custom-call(bf16[256,2048]{1,0:T(8,128)(2,1)} %bitcast.12, s32[6,1,256]{2,1,0:T(1,128)} %bitcast.13, s32[6,1,256]{2,1,0:T(1,128)} %bitcast.14, f32[6,1,256]{2,1,0:T(1,128)} %bitcast.15, bf16[2,2048,1408]{2,1,0:T(8,128)(2,1)} %wg.1, bf16[2,2048,1408]{2,1,0:T(8,128)(2,1)} %wu.1, bf16[2,1408,2048]{2,1,0:T(8,128)(2,1)} %wd.1, ...), custom_call_target="tpu_custom_call" | custom-call | tf_op jit(solution)/shard_map/moe/pallas_call | solution.py:446
  140.6 2.3 %copy.12 = bf16[1,1,256,2048]{3,2,1,0:T(8,128)(2,1)} copy(bf16[1,1,256,2048]{3,2,1,0:T(8,128)(2,1)} %bitcast.11) | data formatting | bytes 2097152

commit v3 on v2

--- a/solution.py
+++ b/solution.py
@@ -251,16 +251,15 @@
             pl.semaphore_signal(barrier, inc=1, device_id={"ep": peer}, device_id_type=MESH)
     with scope("x_in"):
         done(inputs)
-        pl.semaphore_wait(barrier, len(peers))
-        for k in range(2):
-            start(("x", ON, k), ("x", BACK, k))
         for t in range(ahead):
             go(up_tile(0, t))
+        pl.semaphore_wait(barrier, len(peers))
+        start(("x", ON, 0), ("x", BACK, 0))
     with scope("routing"):
         routing()
         if full > unit:
             r[:, pl.ds(unit, full - unit), :] = jnp.zeros((units, full - unit, d), BF16)
-        start(("m", ON), ("m", BACK), ("m", FAR))
+        start(("m", FAR), ("x", ON, 1), ("x", BACK, 1), ("m", ON), ("m", BACK))
 
     with scope("shared_up"):
         ups(0, lambda e: xg[HERE])
@@ -272,10 +271,11 @@
         for i in (ON, BACK):
             arrived(("x", i, 0))
             start(("xx", i))
+    with scope("shared_down"):
+        downs(0, shared_store)
+    with scope("wait_mm"):
         arrived(("m", FAR))
         start("mm")
-    with scope("shared_down"):
-        downs(0, shared_store)
     with scope("x_rest"):
         for i in (ON, BACK):
             arrived(("x", i, 1), ("m", i))

time: 143 us -> 140 us (0.979)
  Pallas kernels: 141 us -> 137 us
    pallas_call x1, Pallas kernels: 141 us -> 137 us  [local(): pl.pallas_call(functools.partial(kernel, side, slots), out_shape=jax.Shap...]
where the time goes in v3:
time: 140 us; the launch traced here: 139 us
  Pallas kernels  137 us (98%)
  local copies, waits for them, and re-layouts  2.3 us (2%)
    pallas_call x1, Pallas kernels, local(): pl.pallas_call(functools.partial(kernel, side, slots), out_shape=jax.Shap...  137 us

profile of v3, /device:TPU:98, one launch (start us, length us, event | category | flops | bytes accessed | tf_op | source)
XLA Modules:
  0.0 139.5 jit_solution(12480709117215384915)
XLA Ops:
  0.0 137.2 %moe.1 = bf16[256,2048]{1,0:T(8,128)(2,1)} custom-call(bf16[256,2048]{1,0:T(8,128)(2,1)} %bitcast.12, s32[6,1,256]{2,1,0:T(1,128)} %bitcast.13, s32[6,1,256]{2,1,0:T(1,128)} %bitcast.14, f32[6,1,256]{2,1,0:T(1,128)} %bitcast.15, bf16[2,2048,1408]{2,1,0:T(8,128)(2,1)} %wg.1, bf16[2,2048,1408]{2,1,0:T(8,128)(2,1)} %wu.1, bf16[2,1408,2048]{2,1,0:T(8,128)(2,1)} %wd.1, ...), custom_call_target="tpu_custom_call" | custom-call | tf_op jit(solution)/shard_map/moe/pallas_call | solution.py:446
  137.2 2.3 %copy.12 = bf16[1,1,256,2048]{3,2,1,0:T(8,128)(2,1)} copy(bf16[1,1,256,2048]{3,2,1,0:T(8,128)(2,1)} %bitcast.11) | data formatting | bytes 2097152

commit v4 on v3

--- a/solution.py
+++ b/solution.py
@@ -17,7 +17,7 @@
 LANE = 128
 WIDE = 2 * LANE
 BUFFERS = 6
-COPIES = 34
+COPIES = 58
 BF16, F32 = jnp.bfloat16, jnp.float32
 scope = contextlib.nullcontext
 
@@ -31,8 +31,8 @@
     return (g * jax.nn.sigmoid(g) * u).astype(BF16)
 
 
-def kernel(side, slots, x_hbm, expert_hbm, slot_hbm, gate_hbm, wg, wu, wd, sg, su, sd, y_ref,
-           expert_ref, slot_ref, gate_ref, xg, mg, column, onehot, combine, sent, fwd, z, r, fwdb, h, w, part, near, rfar, rn, ysh,
+def kernel(side, slots, x_hbm, expert_hbm, slot_hbm, gate_hbm, wg, wu, wd, sg, su, sd, y_hbm,
+           expert_ref, slot_ref, gate_ref, xg, mg, column, onehot, ybuf, sent, fwd, z, r, fwdb, h, w, part, near, rfar, rn, ysh,
            in_sem, w_sem, send_sem, recv_sem):
     tokens, d = x_hbm.shape
     per, _, ff = wg.shape
@@ -62,6 +62,12 @@
             device_id={"ep": to}, device_id_type=MESH)
 
     lo, hi, body = pl.ds(0, half), pl.ds(half, half), pl.ds(0, unit)
+    sides = pl.ds(0, d // 2), pl.ds(d // 2, d // 2)
+    spans = [(e * group + (-e * group) % 16, (e * group + FAR * slots) // 16 * 16) for e in range(per)]
+    free = len(spans)
+    spans += [(spans[e][1], spans[e + 1][0] if e + 1 < per else unit) for e in range(per)]
+    assert spans[0][0] == 0
+    early = ((FAR, SAME), (FAR, OTHER), (ON, SAME), (BACK, SAME))
     c = {}
 
     def link(name, src, dst, to):
@@ -77,23 +83,34 @@
         link(("xx", i), xg.at[i, first], xg.at[FAR, first], at(way, 0, SAME))
     link(("m", FAR), mg.at[HERE, FAR], mg.at[ON, FAR], at(1, 0, SAME))
     link("mm", mg.at[ON, FAR], mg.at[FAR, FAR], at(1, 0, SAME))
-    link(("z", HERE, OTHER), sent.at[HERE, OTHER], z.at[OTHER, HERE], at(0, 0, OTHER))
+    def unit_links(i, j, dst, to):
+        if (i, j) in early:
+            for k, (first, end) in enumerate(spans):
+                these = pl.ds(first, end - first)
+                link(("s", i, j, k), sent.at[i, j, these], dst.at[these], to)
+        else:
+            link(("s", i, j), sent.at[i, j], dst, to)
+
+    unit_links(HERE, OTHER, z.at[OTHER, HERE], at(0, 0, OTHER))
     link(("r", HERE, OTHER), z.at[OTHER, HERE], back(HERE, OTHER), at(0, 0, OTHER))
     for i, way in ((ON, 1), (BACK, -1)):
         for j in (SAME, OTHER):
-            link(("z", i, j), sent.at[i, j], z.at[j, i], at(0, way, j))
+            unit_links(i, j, z.at[j, i], at(0, way, j))
         link(("r", i, SAME), z.at[SAME, i], back(i, SAME), at(0, -way, SAME))
-        link(("r", i, OTHER), z.at[OTHER, i], back(i, OTHER), at(-way, 0, OTHER))
+        for v, cols in enumerate(sides):
+            link(("r", i, OTHER, v), z.at[OTHER, i, :, cols], back(i, OTHER).at[:, cols], at(-way, 0, OTHER))
     for j, way in ((SAME, 1), (OTHER, -1)):
-        link(("f", j), sent.at[FAR, j], fwd.at[j], at(0, way, SAME))
+        unit_links(FAR, j, fwd.at[j], at(0, way, SAME))
         link(("z", FAR, j), fwd.at[j], z.at[j, FAR], at(0, way, j))
-        link(("r", FAR, j), fwdb.at[j], back(FAR, j), at(0, -way, SAME))
-    link(("g", SAME), z.at[SAME, FAR], fwdb.at[SAME], at(0, -1, SAME))
-    link(("g", OTHER), z.at[OTHER, FAR], fwdb.at[OTHER], at(1, 0, OTHER))
+        for v, cols in enumerate(sides):
+            to = at(0, -1, SAME) if j == SAME else at(1, 0, OTHER)
+            link(("g", j, v), z.at[j, FAR, :, cols], fwdb.at[j, :, cols], to)
+            link(("r", FAR, j, v), fwdb.at[j, :, cols], back(FAR, j).at[:, cols], at(0, -way, SAME))
     for k, way, first, second in ((0, 1, lo, hi), (1, -1, hi, lo)):
-        link(("pp", k), part.at[2, first], rfar.at[k], at(way, 0, SAME))
-        link(("p", k, 0), part.at[k, second], rn.at[k, second], at(way, 0, SAME))
-        link(("p", k, 1), part.at[k, first], rn.at[k, first], at(way, 0, SAME))
+        for v, cols in enumerate(sides):
+            link(("pp", k, v), part.at[2, first, cols], rfar.at[k, :, cols], at(way, 0, SAME))
+            link(("p", k, 0, v), part.at[k, second, cols], rn.at[k, second, cols], at(way, 0, SAME))
+            link(("p", k, 1, v), part.at[k, first, cols], rn.at[k, first, cols], at(way, 0, SAME))
     assert len(c) == COPIES
 
     def start(*which):
@@ -178,8 +195,8 @@
 
         some((jnp.int32(n_up - 1),))
 
-    def downs(p, store):
-        @pl.loop(0, n_down // 2)
+    def downs(p, store, begin=0, end=n_down // 2):
+        @pl.loop(begin, end)
         def _(i):
             ts = (n_up + 2 * i, n_up + 2 * i + 1)
             for t in ts:
@@ -196,7 +213,7 @@
             return jnp.concatenate([z[*a, these, :], z[*b, these, :]], axis=0)
         ups(p, lhs)
 
-    def expert_downs(p, a, b):
+    def expert_downs(p, a, b, *which):
         def store(cols, first, second):
             for k, ref in enumerate((a, b)):
                 v, u = (o[k * rows:(k + 1) * rows] for o in (first, second))
@@ -205,7 +222,7 @@
                 ref[pl.ds(0, last), cols] = v[:last].astype(BF16)
                 ref[pl.ds(last, rows - last), cols] = edge.astype(BF16)
                 ref[pl.ds(rows, last), cols] = u[rows - last:].astype(BF16)
-        downs(p, store)
+        downs(p, store, *which)
 
     def routing():
         def place(to, here):
@@ -292,56 +309,80 @@
 
     step = min(d, 8 * LANE)
 
-    def gather(i, j, out, first=HERE, end=OFFSETS):
+    def gather(i, j, out, end=OFFSETS):
         begin = index[i, j] * full
         lane = lax.broadcasted_iota(jnp.int32, (unit, tokens), 1).astype(F32) + 1.0
-        for s in range(first, end):
+        for s in range(end):
             token = column[pl.ds(begin, unit), s:s + 1]
             onehot[:, pl.ds(s * tokens, tokens)] = jnp.where(lane == token, 1.0, 0.0).astype(BF16)
-        these = pl.ds(first * tokens, (end - first) * tokens)
+        these = pl.ds(0, end * tokens)
 
         @pl.loop(0, d // step)
         def _(k):
             cols = pl.ds(pl.multiple_of(k * step, step), step)
-            v = dot(onehot[:, these], xg[first:end, :, cols].reshape((end - first) * tokens, step))
-            if first > HERE:
-                v = v + out[:, cols].astype(F32)
-            out[:, cols] = v.astype(BF16)
-
-    early = ((FAR, SAME), (FAR, OTHER), (ON, SAME), (BACK, SAME))
+            out[:, cols] = dot(onehot[:, these], xg[:end, :, cols].reshape(end * tokens, step)).astype(BF16)
+
+    def gather_far(i, j, out):
+        begin, late = index[i, j] * full, spans[free:]
+        token = jnp.concatenate(
+            [column[pl.ds(begin + first, end - first), FAR:FAR + 1] for first, end in late], axis=0)
+        lane = lax.broadcasted_iota(jnp.int32, (token.shape[0], tokens), 1).astype(F32) + 1.0
+        onehot[pl.ds(0, token.shape[0]), pl.ds(0, tokens)] = jnp.where(lane == token, 1.0, 0.0).astype(BF16)
+
+        @pl.loop(0, d // step)
+        def _(k):
+            cols = pl.ds(pl.multiple_of(k * step, step), step)
+            v, done_rows = dot(onehot[pl.ds(0, token.shape[0]), pl.ds(0, tokens)], xg[FAR, :, cols]), 0
+            for first, end in late:
+                n = end - first
+                these = pl.ds(first, n)
+                out[these, cols] = (v[done_rows:done_rows + n] + out[these, cols].astype(F32)).astype(BF16)
+                done_rows += n
+
     with scope("gather_early"):
         tables((HERE, ON, BACK))
         for i, j in early:
             gather(i, j, sent.at[i, j], end=FAR)
+            start(*(("s", i, j, k) for k in range(free)))
     with scope("xx_wait"):
         arrived(("xx", ON), ("xx", BACK), "mm")
     with scope("tables"):
         tables(range(OFFSETS))
     for i, j in early:
         with scope("gather_far"):
-            gather(i, j, sent.at[i, j], first=FAR)
-        start(("f", j) if i == FAR else ("z", i, j))
+            gather_far(i, j, sent.at[i, j])
+        start(*(("s", i, j, k) for k in range(free, len(spans))))
     with scope("gather"):
         gather(HERE, OTHER, sent.at[HERE, OTHER])
-        start(("z", HERE, OTHER))
+        start(("s", HERE, OTHER))
         gather(HERE, SAME, z.at[SAME, HERE])
         gather(ON, OTHER, sent.at[ON, OTHER])
         gather(BACK, OTHER, sent.at[BACK, OTHER])
 
+    def all_of(i, j):
+        return [("s", i, j, k) for k in range(len(spans))]
+
     with scope("wait_here"):
-        arrived(("z", HERE, OTHER))
+        arrived(("s", HERE, OTHER))
     with scope("ffn_here_up"):
         expert_ups(1, (SAME, HERE), (OTHER, HERE))
     with scope("wait_f"):
         for j in (SAME, OTHER):
-            arrived(("f", j))
+            arrived(*all_of(FAR, j))
             start(("z", FAR, j))
-    start(("z", ON, OTHER), ("z", BACK, OTHER))
+    start(("s", ON, OTHER), ("s", BACK, OTHER))
     with scope("ffn_here_down"):
         expert_downs(1, r.at[index[HERE, SAME]], z.at[OTHER, HERE])
     start(("r", HERE, OTHER))
+    with scope("weigh"):
+        before = [("x", i, k) for i in (ON, BACK) for k in range(2)] + [("xx", ON), ("xx", BACK)]
+        for name in before:
+            c[name].wait_send()
+        for s in range(OFFSETS):
+            token = lax.broadcasted_iota(jnp.int32, (tokens, total), 0).astype(F32) + 1.0
+            xg[s] = jnp.where(token == table(s), table(s, 1), 0.0).astype(BF16)
     with scope("wait_same"):
-        arrived(("z", ON, SAME), ("z", BACK, SAME))
+        arrived(*all_of(ON, SAME), *all_of(BACK, SAME))
     with scope("ffn_same"):
         expert_ups(2, (SAME, ON), (SAME, BACK))
         expert_downs(2, z.at[SAME, ON], z.at[SAME, BACK])
@@ -350,82 +391,76 @@
         arrived(("z", FAR, SAME), ("z", FAR, OTHER))
     with scope("ffn_far"):
         expert_ups(3, (SAME, FAR), (OTHER, FAR))
-        expert_downs(3, z.at[SAME, FAR], z.at[OTHER, FAR])
-    start(("g", SAME), ("g", OTHER))
+        for v in range(2):
+            expert_downs(3, z.at[SAME, FAR], z.at[OTHER, FAR], v * n_down // 4, (v + 1) * n_down // 4)
+            start(("g", SAME, v), ("g", OTHER, v))
     with scope("wait_other"):
-        arrived(("z", ON, OTHER), ("z", BACK, OTHER))
-    with scope("ffn_other_up"):
+        arrived(("s", ON, OTHER), ("s", BACK, OTHER))
+    with scope("ffn_other"):
         expert_ups(4, (OTHER, ON), (OTHER, BACK))
-    with scope("ffn_other_down"):
-        expert_downs(4, z.at[OTHER, ON], z.at[OTHER, BACK])
-    start(("r", ON, OTHER), ("r", BACK, OTHER))
+        for v in range(2):
+            expert_downs(4, z.at[OTHER, ON], z.at[OTHER, BACK], v * n_down // 4, (v + 1) * n_down // 4)
+            if v == 0:
+                start(("r", ON, OTHER, v), ("r", BACK, OTHER, v))
     with scope("wait_g"):
-        for j in (SAME, OTHER):
-            arrived(("g", j))
-            start(("r", FAR, j))
-    with scope("wait_r_near"):
-        arrived(*(("r", i, j) for i, j in UNITS[1:] if i != FAR))
-
-    def weigh(s):
-        token = lax.broadcasted_iota(jnp.int32, (tokens, total), 0).astype(F32) + 1.0
-        combine[...] = jnp.where(token == table(s), table(s, 1), 0.0).astype(BF16)
-
-    def add_up(store, first=0, end=units):
+        for v in range(2):
+            for j in (SAME, OTHER):
+                arrived(("g", j, v))
+                start(("r", FAR, j, v))
+            if v == 0:
+                start(("r", ON, OTHER, 1), ("r", BACK, OTHER, 1))
+
+    def add_up(s, v, first=0, end=units):
+        cols = sides[v]
         these = pl.ds(first * full, (end - first) * full)
-
-        @pl.loop(0, d // step)
-        def _(k):
-            cols = pl.ds(pl.multiple_of(k * step, step), step)
-            store(cols, dot(combine[:, these], r[first:end, :, cols].reshape((end - first) * full, step)))
-
-    def begin_far(cols, o):
-        near[0, :, cols] = o[:half]
-        near[1, :, cols] = o[half:]
-
-    def keep_far(cols, o):
-        part[2, lo, cols] = (near[0, :, cols] + o[:half]).astype(BF16)
-        part[2, hi, cols] = (near[1, :, cols] + o[half:]).astype(BF16)
-
-    def keep_next(cols, o):
-        near[0, :, cols] = o[:half]
-        part[0, hi, cols] = o[half:].astype(BF16)
-
-    def keep_back(cols, o):
-        near[1, :, cols] = o[half:]
-        part[1, lo, cols] = o[:half].astype(BF16)
-
-    def keep_own(cols, o):
-        ysh[:, cols] = ysh[:, cols] + o
-
-    with scope("sum_far_early"):
-        weigh(FAR)
-        add_up(begin_far, end=index[FAR, SAME])
-    with scope("wait_r_far"):
-        arrived(("r", FAR, SAME), ("r", FAR, OTHER))
-    with scope("sum_far"):
-        add_up(keep_far, first=index[FAR, SAME])
-    start(("pp", 0), ("pp", 1))
-    with scope("sum_near"):
-        weigh(BACK)
-        add_up(keep_next)
-        start(("p", 0, 0))
-        weigh(ON)
-        add_up(keep_back)
-        start(("p", 1, 0))
-    with scope("wait_pp"):
-        for k, first in ((0, lo), (1, hi)):
-            arrived(("pp", k))
-            part[k, first, :] = (near[k] + rfar[k].astype(F32)).astype(BF16)
-            start(("p", k, 1))
-    with scope("sum_own"):
-        weigh(HERE)
-        add_up(keep_own)
-    with scope("wait_p"):
-        arrived(*(("p", k, v) for k in range(2) for v in range(2)))
-    with scope("leave"):
-        y_ref[...] = (ysh[...] + (rn[0].astype(F32) + rn[1].astype(F32))).astype(y_ref.dtype)
-        for one in c.values():
-            one.wait_send()
+        return dot(xg[s, :, these], r[first:end, :, cols].reshape((end - first) * full, d // 2))
+
+    with scope("wait_r_same"):
+        arrived(("r", HERE, OTHER), ("r", ON, SAME), ("r", BACK, SAME))
+    for v, cols in enumerate(sides):
+        with scope("wait_r_other"):
+            arrived(("r", ON, OTHER, v), ("r", BACK, OTHER, v))
+        with scope("sum_far_early"):
+            o = add_up(FAR, v, end=index[FAR, SAME])
+            near[0, :, cols] = o[:half]
+            near[1, :, cols] = o[half:]
+        with scope("wait_r_far"):
+            arrived(("r", FAR, SAME, v), ("r", FAR, OTHER, v))
+        with scope("sum_far"):
+            o = add_up(FAR, v, first=index[FAR, SAME])
+            part[2, lo, cols] = (near[0, :, cols] + o[:half]).astype(BF16)
+            part[2, hi, cols] = (near[1, :, cols] + o[half:]).astype(BF16)
+        start(("pp", 0, v), ("pp", 1, v))
+        with scope("sum_near"):
+            o = add_up(BACK, v)
+            near[0, :, cols] = o[:half]
+            part[0, hi, cols] = o[half:].astype(BF16)
+            start(("p", 0, 0, v))
+            o = add_up(ON, v)
+            near[1, :, cols] = o[half:]
+            part[1, lo, cols] = o[:half].astype(BF16)
+            start(("p", 1, 0, v))
+        with scope("sum_own"):
+            ysh[:, cols] = ysh[:, cols] + add_up(HERE, v)
+        with scope("wait_pp"):
+            for k, first in ((0, lo), (1, hi)):
+                arrived(("pp", k, v))
+                part[k, first, cols] = (near[k, :, cols] + rfar[k, :, cols].astype(F32)).astype(BF16)
+                start(("p", k, 1, v))
+    outputs = []
+    for v, cols in enumerate(sides):
+        with scope("wait_p"):
+            arrived(*(("p", k, n, v) for k in range(2) for n in range(2)))
+        with scope("leave"):
+            y = ysh[:, cols] + (rn[0, :, cols].astype(F32) + rn[1, :, cols].astype(F32))
+            ybuf[:, cols] = y.astype(BF16)
+            outputs.append(pltpu.make_async_copy(ybuf.at[:, cols], y_hbm.at[:, cols], in_sem.at[4 + v]))
+            go(outputs[v:])
+    with scope("end"):
+        for name, one in c.items():
+            if name not in before:
+                one.wait_send()
+        done(outputs)
 
 
 def solution(mesh):
@@ -442,19 +477,19 @@
         full = unit + (-unit) % LANE
         half, units = tokens // 2, len(UNITS)
         choices = (v.transpose(0, 3, 1, 2).reshape(top, 1, tokens) for v in (expert, slot, gate))
-        anywhere, vmem = pl.BlockSpec(memory_space=pl.ANY), pl.BlockSpec(memory_space=pltpu.VMEM)
+        anywhere = pl.BlockSpec(memory_space=pl.ANY)
         y = pl.pallas_call(
             functools.partial(kernel, side, slots),
             out_shape=jax.ShapeDtypeStruct((tokens, d), x.dtype),
             in_specs=[anywhere] * 10,
-            out_specs=vmem,
+            out_specs=anywhere,
             scratch_shapes=[
                 *(pltpu.VMEM((top, 1, tokens), v.dtype) for v in (expert, slot, gate)),
                 pltpu.VMEM((OFFSETS, tokens, d), BF16),
                 pltpu.VMEM((OFFSETS, OFFSETS, 2, units * full), F32),
                 pltpu.VMEM((units * full, 2 * OFFSETS), F32),
                 pltpu.VMEM((unit, OFFSETS * tokens), BF16),
-                pltpu.VMEM((tokens, units * full), BF16),
+                pltpu.VMEM((tokens, d), BF16),
                 pltpu.VMEM((OFFSETS, 2, unit, d), BF16),
                 pltpu.VMEM((2, unit, d), BF16),
                 pltpu.VMEM((2, OFFSETS, unit, d), BF16),
@@ -467,7 +502,7 @@
                 pltpu.VMEM((2, half, d), BF16),
                 pltpu.VMEM((2, tokens, d), BF16),
                 pltpu.VMEM((tokens, d), F32),
-                pltpu.SemaphoreType.DMA((4,)),
+                pltpu.SemaphoreType.DMA((6,)),
                 pltpu.SemaphoreType.DMA((BUFFERS, 4)),
                 pltpu.SemaphoreType.DMA((COPIES,)),
                 pltpu.SemaphoreType.DMA((COPIES,)),

time: 140 us -> 133 us (0.950)
  Pallas kernels: 137 us -> 129 us
    pallas_call x1, Pallas kernels: 137 us -> 129 us  [local(): pl.pallas_call(functools.partial(kernel, side, slots), out_shape=jax.Shap...]
where the time goes in v4:
time: 133 us; the launch traced here: 132 us
  Pallas kernels  129 us (97%)
  local copies, waits for them, and re-layouts  2.3 us (2%)
    pallas_call x1, Pallas kernels, local(): pl.pallas_call(functools.partial(kernel, side, slots), out_shape=jax.Shap...  129 us

profile of v4, /device:TPU:98, one launch (start us, length us, event | category | flops | bytes accessed | tf_op | source)
XLA Modules:
  0.0 131.6 jit_solution(9218680994429486795)
XLA Ops:
  0.0 129.3 %moe.1 = bf16[256,2048]{1,0:T(8,128)(2,1)} custom-call(bf16[256,2048]{1,0:T(8,128)(2,1)} %bitcast.12, s32[6,1,256]{2,1,0:T(1,128)} %bitcast.13, s32[6,1,256]{2,1,0:T(1,128)} %bitcast.14, f32[6,1,256]{2,1,0:T(1,128)} %bitcast.15, bf16[2,2048,1408]{2,1,0:T(8,128)(2,1)} %wg.1, bf16[2,2048,1408]{2,1,0:T(8,128)(2,1)} %wu.1, bf16[2,1408,2048]{2,1,0:T(8,128)(2,1)} %wd.1, ...), custom_call_target="tpu_custom_call" | custom-call | tf_op jit(solution)/shard_map/moe/pallas_call | solution.py:481
  129.3 2.3 %copy.12 = bf16[1,1,256,2048]{3,2,1,0:T(8,128)(2,1)} copy(bf16[1,1,256,2048]{3,2,1,0:T(8,128)(2,1)} %bitcast.11) | data formatting | bytes 2097152

commit v5 on v4

--- a/solution.py
+++ b/solution.py
@@ -17,7 +17,7 @@
 LANE = 128
 WIDE = 2 * LANE
 BUFFERS = 6
-COPIES = 58
+SENDS, LANDINGS = 9, 25
 BF16, F32 = jnp.bfloat16, jnp.float32
 scope = contextlib.nullcontext
 
@@ -31,8 +31,8 @@
     return (g * jax.nn.sigmoid(g) * u).astype(BF16)
 
 
-def kernel(side, slots, x_hbm, expert_hbm, slot_hbm, gate_hbm, wg, wu, wd, sg, su, sd, y_hbm,
-           expert_ref, slot_ref, gate_ref, xg, mg, column, onehot, ybuf, sent, fwd, z, r, fwdb, h, w, part, near, rfar, rn, ysh,
+def kernel(side, slots, x_hbm, expert_hbm, slot_hbm, gate_hbm, wg, wu, wd, sg, su, sd, y_ref,
+           expert_ref, slot_ref, gate_ref, xg, mg, column, onehot, sent, fwd, z, r, fwdb, h, w, part, near, rfar, rn, ysh,
            in_sem, w_sem, send_sem, recv_sem):
     tokens, d = x_hbm.shape
     per, _, ff = wg.shape
@@ -56,11 +56,6 @@
         a, b = lax.rem(pa + da + side, side), lax.rem(pb + db + side, side)
         return sa * a + sb * b + (1 - core if other else core)
 
-    def copy(i, src, dst, to):
-        return pltpu.make_async_remote_copy(
-            src_ref=src, dst_ref=dst, send_sem=send_sem.at[i], recv_sem=recv_sem.at[i],
-            device_id={"ep": to}, device_id_type=MESH)
-
     lo, hi, body = pl.ds(0, half), pl.ds(half, half), pl.ds(0, unit)
     sides = pl.ds(0, d // 2), pl.ds(d // 2, d // 2)
     spans = [(e * group + (-e * group) % 16, (e * group + FAR * slots) // 16 * 16) for e in range(per)]
@@ -68,58 +63,73 @@
     spans += [(spans[e][1], spans[e + 1][0] if e + 1 < per else unit) for e in range(per)]
     assert spans[0][0] == 0
     early = ((FAR, SAME), (FAR, OTHER), (ON, SAME), (BACK, SAME))
-    c = {}
-
-    def link(name, src, dst, to):
-        c[name] = copy(len(c), src, dst, to)
+    c, sends, landings = {}, {}, {}
+
+    def link(name, src, dst, to, out, into):
+        c[name] = pltpu.make_async_remote_copy(
+            src_ref=src, dst_ref=dst, send_sem=send_sem.at[sends.setdefault(out, len(sends))],
+            recv_sem=recv_sem.at[landings.setdefault(into, len(landings))],
+            device_id={"ep": to}, device_id_type=MESH)
 
     def back(i, j):
         return r.at[index[i, j], body]
 
     for i, way, first, second in ((ON, 1, lo, hi), (BACK, -1, hi, lo)):
-        link(("x", i, 0), xg.at[HERE, first], xg.at[i, first], at(way, 0, SAME))
-        link(("x", i, 1), xg.at[HERE, second], xg.at[i, second], at(way, 0, SAME))
-        link(("m", i), mg.at[HERE, i], mg.at[i, i], at(way, 0, SAME))
-        link(("xx", i), xg.at[i, first], xg.at[FAR, first], at(way, 0, SAME))
-    link(("m", FAR), mg.at[HERE, FAR], mg.at[ON, FAR], at(1, 0, SAME))
-    link("mm", mg.at[ON, FAR], mg.at[FAR, FAR], at(1, 0, SAME))
-    def unit_links(i, j, dst, to):
+        link(("x", i, 0), xg.at[HERE, first], xg.at[i, first], at(way, 0, SAME), "x", ("x", i, 0))
+        link(("x", i, 1), xg.at[HERE, second], xg.at[i, second], at(way, 0, SAME), "x", ("x", i, 1))
+        link(("xx", i), xg.at[i, first], xg.at[FAR, first], at(way, 0, SAME), "x", "xx")
+        link(("m", i), mg.at[HERE, i], mg.at[i, i], at(way, 0, SAME), "m", ("m", i))
+    link(("m", FAR), mg.at[HERE, FAR], mg.at[ON, FAR], at(1, 0, SAME), "m", ("m", FAR))
+    link("mm", mg.at[ON, FAR], mg.at[FAR, FAR], at(1, 0, SAME), "m", "mm")
+
+    def unit_links(i, j, dst, to, out, into):
         if (i, j) in early:
             for k, (first, end) in enumerate(spans):
                 these = pl.ds(first, end - first)
-                link(("s", i, j, k), sent.at[i, j, these], dst.at[these], to)
+                link(("s", i, j, k), sent.at[i, j, these], dst.at[these], to, out, into)
         else:
-            link(("s", i, j), sent.at[i, j], dst, to)
-
-    unit_links(HERE, OTHER, z.at[OTHER, HERE], at(0, 0, OTHER))
-    link(("r", HERE, OTHER), z.at[OTHER, HERE], back(HERE, OTHER), at(0, 0, OTHER))
+            link(("s", i, j), sent.at[i, j], dst, to, out, into)
+
+    unit_links(HERE, OTHER, z.at[OTHER, HERE], at(0, 0, OTHER), "s_here", "s_here")
+    link(("r", HERE, OTHER), z.at[OTHER, HERE], back(HERE, OTHER), at(0, 0, OTHER), ("z", OTHER), "r")
     for i, way in ((ON, 1), (BACK, -1)):
         for j in (SAME, OTHER):
-            unit_links(i, j, z.at[j, i], at(0, way, j))
-        link(("r", i, SAME), z.at[SAME, i], back(i, SAME), at(0, -way, SAME))
+            unit_links(i, j, z.at[j, i], at(0, way, j), "s", ("s", j))
+        link(("r", i, SAME), z.at[SAME, i], back(i, SAME), at(0, -way, SAME), ("z", SAME), "r")
         for v, cols in enumerate(sides):
-            link(("r", i, OTHER, v), z.at[OTHER, i, :, cols], back(i, OTHER).at[:, cols], at(-way, 0, OTHER))
+            link(("r", i, OTHER, v), z.at[OTHER, i, :, cols], back(i, OTHER).at[:, cols], at(-way, 0, OTHER),
+                 ("z", OTHER), ("r", OTHER, v))
     for j, way in ((SAME, 1), (OTHER, -1)):
-        unit_links(FAR, j, fwd.at[j], at(0, way, SAME))
-        link(("z", FAR, j), fwd.at[j], z.at[j, FAR], at(0, way, j))
+        unit_links(FAR, j, fwd.at[j], at(0, way, SAME), "s", "fwd")
+        link(("z", FAR, j), fwd.at[j], z.at[j, FAR], at(0, way, j), "fwd", "z_far")
         for v, cols in enumerate(sides):
             to = at(0, -1, SAME) if j == SAME else at(1, 0, OTHER)
-            link(("g", j, v), z.at[j, FAR, :, cols], fwdb.at[j, :, cols], to)
-            link(("r", FAR, j, v), fwdb.at[j, :, cols], back(FAR, j).at[:, cols], at(0, -way, SAME))
+            link(("g", j, v), z.at[j, FAR, :, cols], fwdb.at[j, :, cols], to, ("z", j), ("g", v))
+            link(("r", FAR, j, v), fwdb.at[j, :, cols], back(FAR, j).at[:, cols], at(0, -way, SAME),
+                 "fwdb", ("r", FAR, v))
     for k, way, first, second in ((0, 1, lo, hi), (1, -1, hi, lo)):
         for v, cols in enumerate(sides):
-            link(("pp", k, v), part.at[2, first, cols], rfar.at[k, :, cols], at(way, 0, SAME))
-            link(("p", k, 0, v), part.at[k, second, cols], rn.at[k, second, cols], at(way, 0, SAME))
-            link(("p", k, 1, v), part.at[k, first, cols], rn.at[k, first, cols], at(way, 0, SAME))
-    assert len(c) == COPIES
+            link(("pp", k, v), part.at[2, first, cols], rfar.at[k, :, cols], at(way, 0, SAME), "part", ("pp", v))
+            for n, these in enumerate((second, first)):
+                link(("p", k, n, v), part.at[k, these, cols], rn.at[k, these, cols], at(way, 0, SAME),
+                     "part", ("p", v))
+    assert len(sends) == SENDS and len(landings) == LANDINGS
 
     def start(*which):
         for i in which:
             c[i].start()
 
-    def arrived(*which):
-        for i in which:
-            c[i].wait_recv()
+    def wait(sem, ref):
+        pltpu.make_async_copy(ref, ref, sem).wait()
+
+    def arrived(into, ref):
+        wait(recv_sem.at[landings[into]], ref)
+
+    def gone(out, ref):
+        wait(send_sem.at[sends[out]], ref)
+
+    near_units = pl.ds(index[HERE, OTHER], 3)
+    other_units, far_units = pl.ds(index[ON, OTHER], 2), pl.ds(index[FAR, SAME], 2)
 
     n_up, n_down, passes = ff // LANE, d // WIDE, 5
     n_tiles = n_up + n_down
@@ -139,7 +149,7 @@
                 else:
                     src = own.at[e, :, pl.ds(pl.multiple_of(t * LANE, LANE), LANE)]
                 out.append(pltpu.make_async_copy(
-                    src, w.at[slot, e, :, pl.ds(k * LANE, LANE)], w_sem.at[slot, len(out)]))
+                    src, w.at[slot, e, :, pl.ds(k * LANE, LANE)], w_sem.at[slot]))
         return out
 
     def down_tile(p, t):
@@ -148,7 +158,7 @@
         out = []
         for e in range(per):
             src = sd.at[pl.ds(e * ff, ff), cols] if p == 0 else wd.at[e, :, cols]
-            out.append(pltpu.make_async_copy(src, w.at[slot, e, pl.ds(0, ff), :], w_sem.at[slot, len(out)]))
+            out.append(pltpu.make_async_copy(src, w.at[slot, e, pl.ds(0, ff), :], w_sem.at[slot]))
         return out
 
     def go(copies):
@@ -181,7 +191,8 @@
     def ups(p, lhs):
         def some(ts):
             for t in ts:
-                done(up_tile(p, t))
+                slot = slot_of(p, t)
+                wait(w_sem.at[slot], w.at[slot])
             for t in ts:
                 fetch_in_up(p, t + ahead)
             for t in ts:
@@ -200,7 +211,8 @@
         def _(i):
             ts = (n_up + 2 * i, n_up + 2 * i + 1)
             for t in ts:
-                done(down_tile(p, t))
+                slot = slot_of(p, t)
+                wait(w_sem.at[slot], w.at[slot, :, pl.ds(0, ff), :])
             for t in ts:
                 fetch_in_down(p, t + ahead)
             for t in ts:
@@ -285,17 +297,18 @@
         ysh[:, cols] = first + second
 
     with scope("x_wait"):
-        for i in (ON, BACK):
-            arrived(("x", i, 0))
+        for i, first in ((ON, lo), (BACK, hi)):
+            arrived(("x", i, 0), xg.at[i, first])
             start(("xx", i))
     with scope("shared_down"):
         downs(0, shared_store)
     with scope("wait_mm"):
-        arrived(("m", FAR))
+        arrived(("m", FAR), mg.at[ON, FAR])
         start("mm")
     with scope("x_rest"):
-        for i in (ON, BACK):
-            arrived(("x", i, 1), ("m", i))
+        for i, second in ((ON, hi), (BACK, lo)):
+            arrived(("x", i, 1), xg.at[i, second])
+            arrived(("m", i), mg.at[i, i])
 
     def table(s, v=0):
         return mg[s, s, v:v + 1, :]
@@ -345,7 +358,8 @@
             gather(i, j, sent.at[i, j], end=FAR)
             start(*(("s", i, j, k) for k in range(free)))
     with scope("xx_wait"):
-        arrived(("xx", ON), ("xx", BACK), "mm")
+        arrived("xx", xg.at[FAR])
+        arrived("mm", mg.at[FAR, FAR])
     with scope("tables"):
         tables(range(OFFSETS))
     for i, j in early:
@@ -359,43 +373,37 @@
         gather(ON, OTHER, sent.at[ON, OTHER])
         gather(BACK, OTHER, sent.at[BACK, OTHER])
 
-    def all_of(i, j):
-        return [("s", i, j, k) for k in range(len(spans))]
-
     with scope("wait_here"):
-        arrived(("s", HERE, OTHER))
+        arrived("s_here", z.at[OTHER, HERE])
     with scope("ffn_here_up"):
         expert_ups(1, (SAME, HERE), (OTHER, HERE))
     with scope("wait_f"):
-        for j in (SAME, OTHER):
-            arrived(*all_of(FAR, j))
-            start(("z", FAR, j))
+        arrived("fwd", fwd)
+        start(("z", FAR, SAME), ("z", FAR, OTHER))
     start(("s", ON, OTHER), ("s", BACK, OTHER))
     with scope("ffn_here_down"):
         expert_downs(1, r.at[index[HERE, SAME]], z.at[OTHER, HERE])
     start(("r", HERE, OTHER))
     with scope("weigh"):
-        before = [("x", i, k) for i in (ON, BACK) for k in range(2)] + [("xx", ON), ("xx", BACK)]
-        for name in before:
-            c[name].wait_send()
+        gone("x", xg.at[pl.ds(0, 3)])
         for s in range(OFFSETS):
             token = lax.broadcasted_iota(jnp.int32, (tokens, total), 0).astype(F32) + 1.0
             xg[s] = jnp.where(token == table(s), table(s, 1), 0.0).astype(BF16)
     with scope("wait_same"):
-        arrived(*all_of(ON, SAME), *all_of(BACK, SAME))
+        arrived(("s", SAME), z.at[SAME, pl.ds(ON, 2)])
     with scope("ffn_same"):
         expert_ups(2, (SAME, ON), (SAME, BACK))
         expert_downs(2, z.at[SAME, ON], z.at[SAME, BACK])
     start(("r", ON, SAME), ("r", BACK, SAME))
     with scope("wait_far"):
-        arrived(("z", FAR, SAME), ("z", FAR, OTHER))
+        arrived("z_far", z.at[:, FAR])
     with scope("ffn_far"):
         expert_ups(3, (SAME, FAR), (OTHER, FAR))
         for v in range(2):
             expert_downs(3, z.at[SAME, FAR], z.at[OTHER, FAR], v * n_down // 4, (v + 1) * n_down // 4)
             start(("g", SAME, v), ("g", OTHER, v))
     with scope("wait_other"):
-        arrived(("s", ON, OTHER), ("s", BACK, OTHER))
+        arrived(("s", OTHER), z.at[OTHER, pl.ds(ON, 2)])
     with scope("ffn_other"):
         expert_ups(4, (OTHER, ON), (OTHER, BACK))
         for v in range(2):
@@ -403,10 +411,9 @@
             if v == 0:
                 start(("r", ON, OTHER, v), ("r", BACK, OTHER, v))
     with scope("wait_g"):
-        for v in range(2):
-            for j in (SAME, OTHER):
-                arrived(("g", j, v))
-                start(("r", FAR, j, v))
+        for v, cols in enumerate(sides):
+            arrived(("g", v), fwdb.at[:, :, cols])
+            start(("r", FAR, SAME, v), ("r", FAR, OTHER, v))
             if v == 0:
                 start(("r", ON, OTHER, 1), ("r", BACK, OTHER, 1))
 
@@ -416,16 +423,16 @@
         return dot(xg[s, :, these], r[first:end, :, cols].reshape((end - first) * full, d // 2))
 
     with scope("wait_r_same"):
-        arrived(("r", HERE, OTHER), ("r", ON, SAME), ("r", BACK, SAME))
+        arrived("r", r.at[near_units, body])
     for v, cols in enumerate(sides):
         with scope("wait_r_other"):
-            arrived(("r", ON, OTHER, v), ("r", BACK, OTHER, v))
+            arrived(("r", OTHER, v), r.at[other_units, body, cols])
         with scope("sum_far_early"):
             o = add_up(FAR, v, end=index[FAR, SAME])
             near[0, :, cols] = o[:half]
             near[1, :, cols] = o[half:]
         with scope("wait_r_far"):
-            arrived(("r", FAR, SAME, v), ("r", FAR, OTHER, v))
+            arrived(("r", FAR, v), r.at[far_units, body, cols])
         with scope("sum_far"):
             o = add_up(FAR, v, first=index[FAR, SAME])
             part[2, lo, cols] = (near[0, :, cols] + o[:half]).astype(BF16)
@@ -443,24 +450,25 @@
         with scope("sum_own"):
             ysh[:, cols] = ysh[:, cols] + add_up(HERE, v)
         with scope("wait_pp"):
+            arrived(("pp", v), rfar.at[:, :, cols])
             for k, first in ((0, lo), (1, hi)):
-                arrived(("pp", k, v))
                 part[k, first, cols] = (near[k, :, cols] + rfar[k, :, cols].astype(F32)).astype(BF16)
                 start(("p", k, 1, v))
-    outputs = []
     for v, cols in enumerate(sides):
         with scope("wait_p"):
-            arrived(*(("p", k, n, v) for k in range(2) for n in range(2)))
+            arrived(("p", v), rn.at[:, :, cols])
         with scope("leave"):
             y = ysh[:, cols] + (rn[0, :, cols].astype(F32) + rn[1, :, cols].astype(F32))
-            ybuf[:, cols] = y.astype(BF16)
-            outputs.append(pltpu.make_async_copy(ybuf.at[:, cols], y_hbm.at[:, cols], in_sem.at[4 + v]))
-            go(outputs[v:])
+            y_ref[:, cols] = y.astype(y_ref.dtype)
     with scope("end"):
-        for name, one in c.items():
-            if name not in before:
-                one.wait_send()
-        done(outputs)
+        gone("m", mg.at[HERE])
+        gone("s_here", sent.at[HERE, OTHER])
+        gone("s", sent.at[pl.ds(ON, 3)])
+        gone("fwd", fwd)
+        gone(("z", SAME), z.at[SAME, pl.ds(ON, 3)])
+        gone(("z", OTHER), z.at[OTHER])
+        gone("fwdb", fwdb)
+        gone("part", part)
 
 
 def solution(mesh):
@@ -480,16 +488,15 @@
         anywhere = pl.BlockSpec(memory_space=pl.ANY)
         y = pl.pallas_call(
             functools.partial(kernel, side, slots),
-            out_shape=jax.ShapeDtypeStruct((tokens, d), x.dtype),
+            out_shape=pltpu.VMEM((tokens, d), x.dtype),
             in_specs=[anywhere] * 10,
-            out_specs=anywhere,
+            out_specs=pl.BlockSpec(memory_space=pltpu.VMEM),
             scratch_shapes=[
                 *(pltpu.VMEM((top, 1, tokens), v.dtype) for v in (expert, slot, gate)),
                 pltpu.VMEM((OFFSETS, tokens, d), BF16),
                 pltpu.VMEM((OFFSETS, OFFSETS, 2, units * full), F32),
                 pltpu.VMEM((units * full, 2 * OFFSETS), F32),
                 pltpu.VMEM((unit, OFFSETS * tokens), BF16),
-                pltpu.VMEM((tokens, d), BF16),
                 pltpu.VMEM((OFFSETS, 2, unit, d), BF16),
                 pltpu.VMEM((2, unit, d), BF16),
                 pltpu.VMEM((2, OFFSETS, unit, d), BF16),
@@ -502,13 +509,13 @@
                 pltpu.VMEM((2, half, d), BF16),
                 pltpu.VMEM((2, tokens, d), BF16),
                 pltpu.VMEM((tokens, d), F32),
-                pltpu.SemaphoreType.DMA((6,)),
-                pltpu.SemaphoreType.DMA((BUFFERS, 4)),
-                pltpu.SemaphoreType.DMA((COPIES,)),
-                pltpu.SemaphoreType.DMA((COPIES,)),
+                pltpu.SemaphoreType.DMA((4,)),
+                pltpu.SemaphoreType.DMA((BUFFERS,)),
+                pltpu.SemaphoreType.DMA((SENDS,)),
+                pltpu.SemaphoreType.DMA((LANDINGS,)),
             ],
             compiler_params=pltpu.CompilerParams(
-                collective_id=0, has_side_effects=True, vmem_limit_bytes=67_000_000),
+                collective_id=0, has_side_effects=True, vmem_limit_bytes=62_500_000),
             name="moe",
         )(x.reshape(tokens, d), *choices, w_gate, w_up, w_down, s_gate, s_up, s_down)
         return y.reshape(x.shape)

time: 133 us -> 131 us (0.985)
  the two profiles are of different devices: /device:TPU:98 before, /device:TPU:97 now
where the time goes in v5:
time: 131 us
  Pallas kernels  130 us (99%)
    pallas_call x1, Pallas kernels, local(): pl.pallas_call(functools.partial(kernel, side, slots), out_shape=pltpu.VM...  130 us

profile of v5, /device:TPU:97, one launch (start us, length us, event | category | flops | bytes accessed | tf_op | source)
XLA Modules:
  0.0 131.2 jit_solution(3498464088330422021)
XLA Ops:
  0.0 130.2 %moe.1 = bf16[256,2048]{1,0:T(8,128)(2,1)S(1)} custom-call(bf16[256,2048]{1,0:T(8,128)(2,1)} %bitcast.12, s32[6,1,256]{2,1,0:T(1,128)} %bitcast.13, s32[6,1,256]{2,1,0:T(1,128)} %bitcast.14, f32[6,1,256]{2,1,0:T(1,128)} %bitcast.15, bf16[2,2048,1408]{2,1,0:T(8,128)(2,1)} %wg.1, bf16[2,2048,1408]{2,1,0:T(8,128)(2,1)} %wu.1, bf16[2,1408,2048]{2,1,0:T(8,128)(2,1)} %wd.1, ...), custom_call_target="tpu_custom_call" | custom-call | tf_op jit(solution)/shard_map/moe/pallas_call | solution.py:489
  130.2 1.0 copy.12

commit v6 on v5

--- a/solution.py
+++ b/solution.py
@@ -16,7 +16,7 @@
 UNITS = ((HERE, SAME), (HERE, OTHER), (ON, SAME), (BACK, SAME), (ON, OTHER), (BACK, OTHER), (FAR, SAME), (FAR, OTHER))
 LANE = 128
 WIDE = 2 * LANE
-BUFFERS = 6
+BUFFERS = 7
 SENDS, LANDINGS = 9, 25
 BF16, F32 = jnp.bfloat16, jnp.float32
 scope = contextlib.nullcontext
@@ -380,9 +380,9 @@
     with scope("wait_f"):
         arrived("fwd", fwd)
         start(("z", FAR, SAME), ("z", FAR, OTHER))
-    start(("s", ON, OTHER), ("s", BACK, OTHER))
     with scope("ffn_here_down"):
         expert_downs(1, r.at[index[HERE, SAME]], z.at[OTHER, HERE])
+    start(("s", ON, OTHER), ("s", BACK, OTHER))
     start(("r", HERE, OTHER))
     with scope("weigh"):
         gone("x", xg.at[pl.ds(0, 3)])
@@ -424,7 +424,8 @@
 
     with scope("wait_r_same"):
         arrived("r", r.at[near_units, body])
-    for v, cols in enumerate(sides):
+    def sum_far(v):
+        cols = sides[v]
         with scope("wait_r_other"):
             arrived(("r", OTHER, v), r.at[other_units, body, cols])
         with scope("sum_far_early"):
@@ -438,6 +439,9 @@
             part[2, lo, cols] = (near[0, :, cols] + o[:half]).astype(BF16)
             part[2, hi, cols] = (near[1, :, cols] + o[half:]).astype(BF16)
         start(("pp", 0, v), ("pp", 1, v))
+
+    def sum_near(v):
+        cols = sides[v]
         with scope("sum_near"):
             o = add_up(BACK, v)
             near[0, :, cols] = o[:half]
@@ -447,13 +451,27 @@
             near[1, :, cols] = o[half:]
             part[1, lo, cols] = o[:half].astype(BF16)
             start(("p", 1, 0, v))
+
+    def sum_own(v):
         with scope("sum_own"):
-            ysh[:, cols] = ysh[:, cols] + add_up(HERE, v)
+            ysh[:, sides[v]] = ysh[:, sides[v]] + add_up(HERE, v)
+
+    def pass_on(v):
+        cols = sides[v]
         with scope("wait_pp"):
             arrived(("pp", v), rfar.at[:, :, cols])
             for k, first in ((0, lo), (1, hi)):
                 part[k, first, cols] = (near[k, :, cols] + rfar[k, :, cols].astype(F32)).astype(BF16)
                 start(("p", k, 1, v))
+
+    sum_far(0)
+    sum_near(0)
+    sum_own(0)
+    sum_far(1)
+    pass_on(0)
+    sum_near(1)
+    sum_own(1)
+    pass_on(1)
     for v, cols in enumerate(sides):
         with scope("wait_p"):
             arrived(("p", v), rn.at[:, :, cols])
@@ -515,7 +533,7 @@
                 pltpu.SemaphoreType.DMA((LANDINGS,)),
             ],
             compiler_params=pltpu.CompilerParams(
-                collective_id=0, has_side_effects=True, vmem_limit_bytes=62_500_000),
+                collective_id=0, has_side_effects=True, vmem_limit_bytes=64_500_000),
             name="moe",
         )(x.reshape(tokens, d), *choices, w_gate, w_up, w_down, s_gate, s_up, s_down)
         return y.reshape(x.shape)

time: 131 us -> 131 us (level)
  the two profiles are of different devices: /device:TPU:97 before, /device:TPU:98 now
where the time goes in v6:
time: 131 us; the launch traced here: 129 us
  Pallas kernels  128 us (98%)
    pallas_call x1, Pallas kernels, local(): pl.pallas_call(functools.partial(kernel, side, slots), out_shape=pltpu.VM...  128 us

profile of v6, /device:TPU:98, one launch (start us, length us, event | category | flops | bytes accessed | tf_op | source)
XLA Modules:
  0.0 128.9 jit_solution(4502477274737768274)
XLA Ops:
  0.0 127.9 %moe.1 = bf16[256,2048]{1,0:T(8,128)(2,1)S(1)} custom-call(bf16[256,2048]{1,0:T(8,128)(2,1)} %bitcast.12, s32[6,1,256]{2,1,0:T(1,128)} %bitcast.13, s32[6,1,256]{2,1,0:T(1,128)} %bitcast.14, f32[6,1,256]{2,1,0:T(1,128)} %bitcast.15, bf16[2,2048,1408]{2,1,0:T(8,128)(2,1)} %wg.1, bf16[2,2048,1408]{2,1,0:T(8,128)(2,1)} %wu.1, bf16[2,1408,2048]{2,1,0:T(8,128)(2,1)} %wd.1, ...), custom_call_target="tpu_custom_call" | custom-call | tf_op jit(solution)/shard_map/moe/pallas_call | solution.py:507
  127.9 1.0 copy.12
